TPU v7x, 32 devices: a whole 2x2x4 slice. The times are simulated.
32 devices in a mesh: aa: 4 (over z), ba: 2 (over y), col: 4 (over x, core).
Axes of the slice: x: 2, y: 2, z: 4, core: 2. Of those that a mesh axis runs over, the one named last changes fastest.
Arguments:
- tokens: bfloat16 [2048, 7168], P(('aa', 'col'), 'ba'), may hold values from -6 to 6
- routing: int32 [2048, 8], P(('aa', 'col')), may hold values from 0 to 15, all different within a row; in each aligned block of 128 rows (0 to 127, 128 to 255, ...) at most 80 rows name the same one
- gate_codes: int32 [2048, 8], P(('aa', 'col')), may hold values from 1 to 65535
- w_gate: bfloat16 [16, 7168, 2048], P(('aa', 'col'), None, 'ba'), may hold values from -0.0625 to 0.0625
- w_up: bfloat16 [16, 7168, 2048], P(('aa', 'col'), None, 'ba'), may hold values from -0.0625 to 0.0625
- w_down: bfloat16 [16, 2048, 7168], P(('aa', 'col'), 'ba'), may hold values from -0.125 to 0.125
Outputs:
- mixed: bfloat16 [2048, 7168], P(('aa', 'col'), 'ba')
Inputs may be any that keep to these rules, and one draw needn't show every extreme that they name: `routing`: within each token group of 128 rows (aligned blocks of the rows), no expert is named more than 80 times, a bound that some block reaches. A token names 8 different experts.
All inputs are finite; a program needn't handle non-finite values.
Results may differ from a plain program's by a relative error of at most 0.014.
Values may be sent and summed in bfloat16 or wider, within the bound.
No kernel may reach another device: no remote copies, remote signals or barrier semaphores. Data moves between devices by JAX's collectives and lax.ppermute only.
A program may use at most 192 MiB of HBM per device.

v0:
```python
import jax
import jax.numpy as jnp
from jax import lax
from jax.sharding import PartitionSpec as P

route_scale = 2.827


def route_tables(routing, experts, slots_each, top):
    flat = routing.reshape(-1)
    onehot = (flat[:, None] == jnp.arange(experts, dtype=jnp.int32)[None, :]).astype(jnp.int32)
    before = jnp.cumsum(onehot, axis=0) - onehot
    pos = jnp.sum(before * onehot, axis=1)
    slot = flat * slots_each + pos
    matched = slot[:, None] == jnp.arange(experts * slots_each, dtype=jnp.int32)[None, :]
    owner = jnp.arange(flat.shape[0], dtype=jnp.int32) // top
    slot_token = jnp.sum(jnp.where(matched, owner[:, None], 0), axis=0)
    live = jnp.any(matched, axis=0)
    return (slot, slot_token.reshape(experts, slots_each), live.reshape(experts, slots_each))


def on_device(tokens, routing, gate_codes, w_gate, w_up, w_down):
    n_aa = lax.axis_size("aa")
    n_col = lax.axis_size("col")
    experts = n_aa * n_col
    tok_rows = tokens.shape[0]
    top = routing.shape[1]
    slots_each = min(tok_rows, 5 * tok_rows * top // (4 * experts))
    slot, slot_token, live = route_tables(routing, experts, slots_each, top)
    codes = gate_codes.astype(jnp.float32)
    weight = route_scale * codes / jnp.sum(codes, axis=1, keepdims=True)
    outgoing = jnp.where(live[:, :, None], tokens[slot_token], jnp.zeros((), jnp.bfloat16))
    gate_local = w_gate[0]
    up_local = w_up[0]
    down_local = w_down[0]
    full_rows = lax.all_gather(
        lax.all_to_all(outgoing, ("aa", "col"), split_axis=0, concat_axis=0, tiled=True),
        "ba",
        axis=2,
        tiled=True,
    )
    sources = full_rows.shape[0]
    count = full_rows.shape[1]
    rows = full_rows.reshape(sources * count, full_rows.shape[2])
    gate = jnp.dot(rows, gate_local, preferred_element_type=jnp.float32)
    upper = jnp.dot(rows, up_local, preferred_element_type=jnp.float32)
    hidden = (jax.nn.silu(gate) * upper).astype(jnp.bfloat16)
    partial_out = jnp.dot(hidden, down_local, preferred_element_type=jnp.float32).astype(
        jnp.bfloat16
    )
    summed = lax.psum_scatter(partial_out, "ba", scatter_dimension=1, tiled=True).astype(
        jnp.float32
    )
    returned = lax.all_to_all(
        summed.astype(jnp.bfloat16).reshape(sources, count, summed.shape[1]),
        ("aa", "col"),
        split_axis=0,
        concat_axis=0,
        tiled=True,
    )
    table = returned.reshape(experts * slots_each, returned.shape[2])
    picked = table[slot].reshape(tok_rows, top, table.shape[1]).astype(jnp.float32)
    mixed = jnp.einsum("tk,tkd->td", weight, picked)
    return mixed.astype(jnp.bfloat16)


def solution(mesh):
    return jax.shard_map(
        on_device,
        mesh=mesh,
        in_specs=(
            P(("aa", "col"), "ba"),
            P(("aa", "col"), None),
            P(("aa", "col"), None),
            P(("aa", "col"), None, "ba"),
            P(("aa", "col"), None, "ba"),
            P(("aa", "col"), "ba", None),
        ),
        out_specs=P(("aa", "col"), "ba"),
        check_vma=False,
    )
```

profile of v0, /device:TPU:11, one launch (start us, length us, event | category | flops | bytes accessed | tf_op | source)
XLA Modules:
  0.0 975.5 jit_solution(377460686479931518)
XLA Ops:
  6.5 0.9 copy.14
  7.4 0.1 eq.39
  7.5 0.1 reshape.111
  7.6 4.5 reduce-window.6
  12.1 0.1 slice.12
  12.2 0.1 copy.16
  12.4 0.1 copy.17
  12.4 0.1 broadcast_add_fusion
  12.6 0.6 copy-done.2
  13.2 0.8 fusion.9
  13.9 0.7 select_reduce_fusion
  14.6 0.1 reshape.113
  14.7 0.1 reshape.120
  14.8 0.1 broadcast_in_dim.33
  14.9 7.9 gather_fusion
  22.8 7.8 broadcast_select_fusion
  30.6 205.6 %all_to_all.10 = bf16[16,80,3584]{2,1,0:T(8,128)(2,1)} all-to-all(bf16[16,80,3584]{2,1,0:T(8,128)(2,1)} %broadcast_select_fusion), channel_id=1, replica_groups=mesh['aa'=4,'ba'=2,'col'=4] {'aa','col'}, dimensions={0} | all-to-all | bytes 18350080 | tf_op jit(solution)/shard_map/all_to_all | solution.py:37
  236.2 0.0 all-gather.2.cloned.1.call-update
  236.2 0.2 reduce-scatter.2.cloned.1.call-start
  236.4 218.7 %all-gather.2.cloned.1.call-done = bf16[16,80,7168]{2,1,0:T(8,128)(2,1)} async-done(((bf16[16,80,3584]{2,1,0:T(8,128)(2,1)}), bf16[16,80,7168]{2,1,0:T(8,128)(2,1)}) %all-gather.2.cloned.1.call-update) | async-done | bytes 18350096 | tf_op jit(solution)/shard_map/all_gather | solution.py:36
  455.1 25.6 %fusion.1 = f32[1280,1024]{1,0:T(8,128)} fusion(bf16[1280,7168]{1,0:T(8,128)(2,1)} %bitcast.55, bf16[1,7168,1024]{2,1,0:T(8,128)(2,1)} %param.10), kind=kOutput, calls=%fused_computation.4 | convolution fusion | flops 18790481920 | bytes 38273024 | tf_op jit(solution)/shard_map/dot_general | solution.py:46
  480.7 24.0 %multiply_convert_fusion = bf16[1280,1024]{1,0:T(8,128)(2,1)S(1)} fusion(f32[1280,1024]{1,0:T(8,128)} %fusion.1, bf16[1280,7168]{1,0:T(8,128)(2,1)S(1)} %bitcast.56, bf16[1,7168,1024]{2,1,0:T(8,128)(2,1)} %param.9), kind=kOutput, calls=%fused_computation.11 | convolution fusion | flops 18798346240 | bytes 40894464 | tf_op jit(solution)/shard_map/dot_general | solution.py:45
  504.7 27.0 %convolution_convert_fusion = bf16[1280,7168]{1,0:T(8,128)(2,1)} fusion(bf16[1280,1024]{1,0:T(8,128)(2,1)S(1)} %multiply_convert_fusion, bf16[1,1024,7168]{2,1,0:T(8,128)(2,1)} %param.11), kind=kOutput, calls=%fused_computation.2 | convolution fusion | flops 18799656960 | bytes 35651584 | tf_op jit(solution)/shard_map/dot_general | solution.py:48
  531.7 206.3 %reduce-scatter.2.cloned.1.call-done = bf16[1280,3584]{1,0:T(8,128)(2,1)} async-done(((bf16[1280,7168]{1,0:T(8,128)(2,1)}), bf16[1280,3584]{1,0:T(8,128)(2,1)}) %reduce-scatter.2.cloned.1.call-update) | async-done | bytes 9175056 | tf_op jit(solution)/shard_map/reduce_scatter | solution.py:51
  737.9 6.6 all-to-all-start.1
  744.6 0.1 copy.18
  744.7 0.1 mul.48
  744.8 0.1 copy.19
  745.0 198.8 %all-to-all-done.1 = bf16[16,80,3584]{2,1,0:T(8,128)(2,1)} async-done(((bf16[16,80,3584]{2,1,0:T(8,128)(2,1)}), bf16[16,80,3584]{2,1,0:T(8,128)(2,1)}, u32[]{:S(2)}, u32[]{:S(2)}) %all-to-all-start.1) | async-done | bytes 9175072 | tf_op jit(solution)/shard_map/all_to_all | solution.py:54
  943.8 18.7 %gather_fusion.1 = bf16[1024,3584]{1,0:T(8,128)(2,1)} fusion(bf16[1280,3584]{1,0:T(8,128)(2,1)} %bitcast.9, s32[1024]{0:T(1024)S(1)} %broadcast_clamp_fusion), kind=kCustom, calls=%fused_computation.1 | custom fusion | bytes 14684160 | tf_op jit(solution)/shard_map/gather | solution.py:62
  962.4 5.1 fusion.5
  967.6 1.0 copy.24
  (27 shorter events, 0.2 us)
Async XLA Ops:
  6.5 8.4 copy-start
  6.5 448.5 %all-gather.2.cloned.1.call-start = ((), (), s32[]{:S(2)}) async-start(), calls=%async_computation.3 | async-start | bytes 27525120 | tf_op jit(solution)/shard_map/all_gather | solution.py:36
  12.6 0.6 copy-start.2
  236.2 501.8 %reduce-scatter.2.cloned.1.call-start = ((), (), s32[]{:S(2)}) async-start(), calls=%async_computation.4 | async-start | bytes 27525120 | tf_op jit(solution)/shard_map/reduce_scatter | solution.py:51
  455.1 25.6 %copy-start.6 = (bf16[16,80,7168]{2,1,0:T(8,128)(2,1)S(1)}, bf16[16,80,7168]{2,1,0:T(8,128)(2,1)}, u32[]{:S(2)}) copy-start(bf16[16,80,7168]{2,1,0:T(8,128)(2,1)} %all-gather.2.cloned.1.call-done) | copy-start | bytes 55050244
  737.9 6.6 copy-start.4
  737.9 6.9 copy-start.5
  737.9 7.0 copy-start.3
  737.9 205.8 %all-to-all-start.1 = ((bf16[16,80,3584]{2,1,0:T(8,128)(2,1)}), bf16[16,80,3584]{2,1,0:T(8,128)(2,1)}, u32[]{:S(2)}, u32[]{:S(2)}) async-start(bf16[16,80,3584]{2,1,0:T(8,128)(2,1)} %bitcast.50), calls=%async_computation.2 | async-start | bytes 18350080 | tf_op jit(solution)/shard_map/all_to_all | solution.py:54
  943.8 24.8 %copy-start.1 = (bf16[128,3584]{1,0:T(8,128)(2,1)S(1)}, bf16[128,3584]{1,0:T(8,128)(2,1)}, u32[]{:S(2)}) copy-start(bf16[128,3584]{1,0:T(8,128)(2,1)} %param.6) | copy-start | bytes 2752516
Sparse Core Ops, SparseCore 0:
  236.3 218.7 all-gather.1
  531.8 206.0 reduce-scatter.1
where the time goes:
time: 976 us; the launch traced here: 975 us
  waiting for transfers between devices  624 us (64%)
  blocking collectives  206 us (21%)
  matrix products  81.7 us (8%)
  local copies, waits for them, and re-layouts  30.1 us (3%)
  other arithmetic  14 us (1%)
  between operations  13.5 us (1%)
    all_gather x1, waiting for transfers between devices, on_device(): lax.all_gather(lax.all_to_all(outgoing, ('aa', 'col'), split_axis=0, conc...  219 us
    reduce_scatter x1, waiting for transfers between devices, on_device(): lax.psum_scatter(partial_out, 'ba', scatter_dimension=1, tiled=True)  206 us
    all_to_all x1, blocking collectives, on_device(): lax.all_to_all(outgoing, ('aa', 'col'), split_axis=0, concat_axis=0, tile...  206 us
    all_to_all x1, waiting for transfers between devices, on_device(): lax.all_to_all(summed.astype(jnp.bfloat16).reshape(sources, count, summed...  199 us
    dot_general x1, matrix products, on_device(): jnp.dot(hidden, down_local, preferred_element_type=jnp.float32)  27 us
    dot_general x1, matrix products, on_device(): upper = jnp.dot(rows, up_local, preferred_element_type=jnp.float32)  25.6 us
    dot_general x1, matrix products, on_device(): gate = jnp.dot(rows, gate_local, preferred_element_type=jnp.float32)  24 us
  transfers between devices with their start and end apart: 3, of which 3 were waited for; matrix products, arithmetic and copies ran while one was open for 0% of the time, Pallas kernels for 0%

commit v1 on v0

v1 whole, which is shorter than its diff:
```python
import functools

import jax
import jax.numpy as jnp
from jax import lax
from jax.experimental import pallas as pl
from jax.experimental.pallas import tpu as pltpu
from jax.sharding import PartitionSpec as P


route_scale = 2.827
n_gathers = 2
n_calls = 4


class Phase:
    def __init__(self, axis, inner, outer_n, inner_n):
        self.axis, self.inner, self.outer_n, self.inner_n = axis, inner, outer_n, inner_n
        self.n = inner_n if inner else outer_n
        place = lax.axis_index(axis)
        self.me = place % inner_n if inner else place // inner_n

    def shift(self, value, step):
        pairs = []
        for out in range(self.outer_n):
            for low in range(self.inner_n):
                if self.inner:
                    to = out * self.inner_n + (low + step) % self.inner_n
                else:
                    to = (out + step) % self.outer_n * self.inner_n + low
                pairs.append((out * self.inner_n + low, to))
        return lax.ppermute(value, self.axis, pairs)

    def gather(self, value):
        return jnp.stack([value] + [self.shift(value, s) for s in range(1, self.n)])

    def ordered(self, value, axis):
        return jnp.take(value, (self.me - jnp.arange(self.n)) % self.n, axis=axis)

    def blocks(self, value, axis, moving):
        if not moving:
            return [lax.index_in_dim(value, s, axis, keepdims=False) for s in range(self.n)]
        return [
            lax.dynamic_index_in_dim(value, (self.me - s) % self.n, axis, keepdims=False)
            for s in range(self.n)
        ]

    def send(self, blocks):
        return [self.shift(blocks[s], self.n - s) for s in range(1, self.n)]


def total_of(own, arrived):
    total = own.astype(jnp.float32)
    for block in arrived:
        total = total + block.astype(jnp.float32)
    return total.astype(jnp.bfloat16)


def hidden_body(steps, place, *refs):
    n_x = len(refs) - 5
    xs = refs[:n_x]
    wg, wu, out, gate, upper = refs[n_x:]
    k = pl.program_id(0)
    x = jnp.concatenate([r[...].reshape(-1, r.shape[-1]) for r in xs], axis=0)
    g = jnp.dot(x, wg[0], preferred_element_type=jnp.float32)
    u = jnp.dot(x, wu[0], preferred_element_type=jnp.float32)

    @pl.when(k == 0)
    def _():
        gate[...] = g
        upper[...] = u

    @pl.when(k > 0)
    def _():
        gate[...] += g
        upper[...] += u

    @pl.when(k == steps - 1)
    def _():
        v = gate[...]
        out[...] = (v / (1.0 + jnp.exp(-v)) * upper[...]).astype(jnp.bfloat16)


def down_body(place, hidden, wd, scale, *outs):
    y = jnp.dot(hidden[...], wd[0], preferred_element_type=jnp.float32)
    y = (y * scale[...]).astype(jnp.bfloat16)
    each = y.shape[0] // len(outs)
    for s, out in enumerate(outs):
        out[0] = y[s * each : (s + 1) * each]


def on_device(tokens, routing, gate_codes, w_gate, w_up, w_down):
    n_aa = lax.axis_size("aa")
    n_ba = lax.axis_size("ba")
    n_col = lax.axis_size("col")
    experts = n_aa * n_col
    n_low = 2 if n_col % 2 == 0 else 1
    n_high = n_col // n_low
    zed = Phase("aa", False, n_aa, 1)
    wide = Phase("col", False, n_high, n_low)
    pair = Phase("col", True, n_high, n_low)
    feat = Phase("ba", False, n_ba, 1)
    mine = lax.axis_index("aa") * n_col + lax.axis_index("col")
    tok_rows, width = tokens.shape
    hidden_n = w_gate.shape[2]
    rows = tok_rows // n_calls
    each = n_aa * n_high * rows
    tall = n_low * each
    block = 896 if width % 896 == 0 else width
    per = width // block
    steps = n_ba * per
    place = jnp.stack([feat.me, pair.me]).astype(jnp.int32)

    codes = gate_codes.astype(jnp.float32)
    weight = route_scale * codes / jnp.sum(codes, axis=1, keepdims=True)
    named = routing[None, :, :] == jnp.arange(experts, dtype=jnp.int32)[:, None, None]
    scores = jnp.sum(jnp.where(named, weight[None, :, :], 0.0), axis=2)
    scores = wide.gather(zed.gather(scores))
    scores = pair.gather(scores)
    own = jnp.arange(experts, dtype=jnp.int32)[:, None] == mine
    scores = jnp.sum(jnp.where(own, scores, 0.0), axis=3)
    scores = wide.ordered(zed.ordered(scores, 2), 1)
    scores = jnp.swapaxes(scores, 1, 2)

    def source(k, place):
        return (place[0] + n_ba - k // per) % n_ba

    def hidden_of(gathered, number):
        specs = [
            pl.BlockSpec(
                (n_aa, 1, n_high, 1, rows, block),
                functools.partial(
                    lambda s, k, place: (0, source(k, place), 0, (place[1] + n_low - s) % n_low, number, k % per), s
                ),
            )
            for s in range(n_low)
        ]
        weights = pl.BlockSpec((1, block, hidden_n), lambda k, place: (0, source(k, place) * per + k % per, 0))
        return pl.pallas_call(
            functools.partial(hidden_body, steps),
            grid_spec=pltpu.PrefetchScalarGridSpec(
                num_scalar_prefetch=1,
                grid=(steps,),
                in_specs=specs + [weights, weights],
                out_specs=pl.BlockSpec((tall, hidden_n), lambda k, place: (0, 0)),
                scratch_shapes=[pltpu.VMEM((tall, hidden_n), jnp.float32)] * 2,
            ),
            out_shape=jax.ShapeDtypeStruct((tall, hidden_n), jnp.bfloat16),
            cost_estimate=pl.CostEstimate(
                flops=4 * tall * n_ba * width * hidden_n,
                transcendentals=tall * hidden_n,
                bytes_accessed=4 * n_ba * width * hidden_n + 2 * tall * n_ba * width,
            ),
            compiler_params=pltpu.CompilerParams(vmem_limit_bytes=48 * 1024 * 1024),
        )(place, *[gathered] * n_low, w_gate, w_up)

    def out_of(hidden, number):
        scale = lax.slice_in_dim(scores, number * rows, (number + 1) * rows, axis=3).reshape(-1, 1)
        return pl.pallas_call(
            down_body,
            grid_spec=pltpu.PrefetchScalarGridSpec(
                num_scalar_prefetch=1,
                grid=(steps,),
                in_specs=[
                    pl.BlockSpec((tall, hidden_n), lambda k, place: (0, 0)),
                    pl.BlockSpec((1, hidden_n, block), lambda k, place: (0, 0, source(k, place) * per + k % per)),
                    pl.BlockSpec((tall, 1), lambda k, place: (0, 0)),
                ],
                out_specs=[pl.BlockSpec((1, each, block), lambda k, place: (k // per, 0, k % per))] * n_low,
            ),
            out_shape=[jax.ShapeDtypeStruct((n_ba, each, width), jnp.bfloat16)] * n_low,
            cost_estimate=pl.CostEstimate(
                flops=2 * tall * n_ba * width * hidden_n,
                transcendentals=0,
                bytes_accessed=2 * n_ba * width * hidden_n + 2 * tall * n_ba * width,
            ),
            compiler_params=pltpu.CompilerParams(vmem_limit_bytes=48 * 1024 * 1024),
        )(place, hidden, w_down, scale)

    def give_back(outs):
        arrived = pair.send(outs)
        yield []
        value = total_of(outs[0], arrived).reshape(n_ba, n_aa, n_high, rows, width)
        middle = width // 256 * 128
        first, second = value[..., :middle], value[..., middle:]
        sides = feat.blocks(first, 0, False)
        walls = wide.blocks(second, 2, True)
        got_a, got_b = feat.send(sides), wide.send(walls)
        yield [value]
        first = total_of(sides[0], got_a)
        second = total_of(walls[0], got_b)
        walls = wide.blocks(first, 1, True)
        sides = feat.blocks(second, 0, False)
        got_a, got_b = wide.send(walls), feat.send(sides)
        yield [first, second]
        value = jnp.concatenate([total_of(walls[0], got_a), total_of(sides[0], got_b)], axis=-1)
        floors = zed.blocks(value, 0, True)
        arrived = zed.send(floors)
        yield [value]
        yield [total_of(floors[0], arrived)]

    each_gather = tok_rows // n_gathers
    gathered = []
    for c in range(n_gathers):
        piece = lax.slice_in_dim(tokens, c * each_gather, (c + 1) * each_gather, axis=0)
        piece = lax.all_gather(piece, ("aa", "ba", "col"), axis=0, tiled=False)
        gathered.append(piece.reshape(n_aa, n_ba, n_high, n_low, each_gather, width))

    def tie(value, others):
        return lax.optimization_barrier((value, *others))[0] if others else value

    per_gather = n_calls // n_gathers
    sums, last = [], {}

    def step(number):
        last[number] = next(sums[number])
        return last[number]

    plan = [((), ()), ((), (0,)), ((1, 0, 1, 0, 1), ()), ((), (2, 0, 1))]
    outs = []
    for number in range(n_calls):
        before, between = plan[number]
        ready = [v for c in before for v in step(c)]
        hidden = hidden_of(tie(gathered[number // per_gather], ready + outs), number % per_gather)
        ready = [v for c in between for v in step(c)]
        outs = list(out_of(tie(hidden, ready), number))
        sums.append(give_back(outs))
        step(number)
    for number in range(n_calls):
        for last[number] in sums[number]:
            pass
    return jnp.concatenate([last[c][0] for c in range(n_calls)], axis=0)


def solution(mesh):
    return jax.shard_map(
        on_device,
        mesh=mesh,
        in_specs=(
            P(("aa", "col"), "ba"),
            P(("aa", "col"), None),
            P(("aa", "col"), None),
            P(("aa", "col"), None, "ba"),
            P(("aa", "col"), None, "ba"),
            P(("aa", "col"), "ba", None),
        ),
        out_specs=P(("aa", "col"), "ba"),
        check_vma=False,
    )
```

time: 976 us -> 482 us (0.49)
  waiting for transfers between devices: 624 us -> 226 us
  blocking collectives: 206 us -> 0 us
  Pallas kernels: 0 us -> 163 us
  matrix products: 81.7 us -> 0 us
  starting transfers between devices: 6.86 us -> 40.6 us
  local copies, waits for them, and re-layouts: 30.1 us -> 13.8 us
    reduce_scatter x1 -> x0, waiting for transfers between devices: 206 us -> none  [on_device(): lax.psum_scatter(partial_out, 'ba', scatter_dimension=1, tiled=True)]
    all_to_all x1 -> x0, blocking collectives: 206 us -> none  [on_device(): lax.all_to_all(outgoing, ('aa', 'col'), split_axis=0, concat_axis=0, tile...]
    all_to_all x1 -> x0, waiting for transfers between devices: 199 us -> none  [on_device(): lax.all_to_all(summed.astype(jnp.bfloat16).reshape(sources, count, summed...]
    pallas_call x0 -> x8, Pallas kernels: none -> 163 us  [the longest x4 104 us: hidden_of(): pl.pallas_call(functools.partial(hidden_body, steps), grid_spec=pltpu.Pre...]
    ppermute x0 -> x37, waiting for transfers between devices: none -> 136 us  [shift(): return lax.ppermute(value, self.axis, pairs)]
    all_gather x1 -> x2, waiting for transfers between devices: 219 us -> 90 us  [on_device(): piece = lax.all_gather(piece, ('aa', 'ba', 'col'), axis=0, tiled=False)]
    dot_general x4 -> x0, matrix products: 81.7 us -> none  [the longest x1 27 us: on_device(): jnp.dot(hidden, down_local, preferred_element_type=jnp.float32)]
    ppermute x0 -> x37, starting transfers between devices: none -> 40.5 us  [shift(): return lax.ppermute(value, self.axis, pairs)]
  transfers between devices with their start and end apart: 3 -> 39, of which waited for: 3 -> 23; matrix products, arithmetic and copies ran while one was open for 0% -> 5% of each run, Pallas kernels for 0% -> 23%
where the time goes in v1:
time: 482 us; the launch traced here: 475 us
  waiting for transfers between devices  226 us (47%)
  Pallas kernels  163 us (34%)
  starting transfers between devices  40.6 us (8%)
  other arithmetic  17.6 us (4%)
  between operations  14 us (3%)
  local copies, waits for them, and re-layouts  13.8 us (3%)
    ppermute x37, waiting for transfers between devices, shift(): return lax.ppermute(value, self.axis, pairs)  136 us
    pallas_call x4, Pallas kernels, hidden_of(): pl.pallas_call(functools.partial(hidden_body, steps), grid_spec=pltpu.Pre...  104 us
    all_gather x2, waiting for transfers between devices, on_device(): piece = lax.all_gather(piece, ('aa', 'ba', 'col'), axis=0, tiled=False)  90 us
    pallas_call x4, Pallas kernels, out_of(): pl.pallas_call(down_body, grid_spec=pltpu.PrefetchScalarGridSpec(num_scal...  58.8 us
    ppermute x37, starting transfers between devices, shift(): return lax.ppermute(value, self.axis, pairs)  40.5 us
    convert_element_type x24, other arithmetic, total_of(): return total.astype(jnp.bfloat16)  13.9 us
  transfers between devices with their start and end apart: 39, of which 23 were waited for; matrix products, arithmetic and copies ran while one was open for 5% of the time, Pallas kernels for 23%

profile of v1, /device:TPU:11, one launch (start us, length us, event | category | flops | bytes accessed | tf_op | source)
XLA Modules:
  0.0 475.4 jit_solution(13557885706621758803)
XLA Ops:
  6.5 2.1 fusion.73
  16.8 2.5 collective-permute-done.3
  19.3 4.0 collective-permute-start.4
  25.9 90.0 %all-gather.5.cloned.1.call-done = bf16[2048,3584]{1,0:T(8,128)(2,1)} async-done(((bf16[64,3584]{1,0:T(8,128)(2,1)}), bf16[2048,3584]{1,0:T(8,128)(2,1)}) %all-gather.5.cloned.1.call-update) | async-done | bytes 14680080 | tf_op jit(solution)/shard_map/all_gather | solution.py:206
  115.9 25.9 %shard_map.64.hidden = bf16[512,1024]{1,0:T(8,128)(2,1)S(1)} custom-call(s32[2]{0:T(128)S(1)} %pad_add_fusion.place, bf16[4,2,2,2,64,3584]{5,4,3,2,1,0:T(8,128)(2,1)} %bitcast.190, bf16[4,2,2,2,64,3584]{5,4,3,2,1,0:T(8,128)(2,1)} %bitcast.191, bf16[1,7168,1024]{2,1,0:T(8,128)(2,1)} %refs_2_.7, bf16[1,7168,1024]{2,1,0:T(8,128)(2,1)} %refs_3_.7), custom_call_target="tpu_custom_call" | custom-call | flops 15032385536 | bytes 36700160 | tf_op jit(solution)/shard_map/pallas_call | solution.py:139
  141.8 14.8 %shard_map.65 = (bf16[2,256,3584]{2,1,0:T(8,128)(2,1)S(1)}, bf16[2,256,3584]{2,1,0:T(8,128)(2,1)}) custom-call(s32[2]{0:T(128)S(1)} %pad_add_fusion.place, bf16[512,1024]{1,0:T(8,128)(2,1)S(1)} %shard_map.64.hidden, bf16[1,1024,7168]{2,1,0:T(8,128)(2,1)} %wd.7, f32[512,1]{1,0:T(8,128)S(1)} %reshape.235.scale), custom_call_target="tpu_custom_call" | custom-call | flops 7516192768 | bytes 22020096 | tf_op jit(solution)/shard_map/pallas_call | solution.py:159
  158.9 26.4 %shard_map.66.hidden = bf16[512,1024]{1,0:T(8,128)(2,1)S(1)} custom-call(s32[2]{0:T(128)S(1)} %pad_add_fusion.place, bf16[4,2,2,2,64,3584]{5,4,3,2,1,0:T(8,128)(2,1)} %bitcast.192, bf16[4,2,2,2,64,3584]{5,4,3,2,1,0:T(8,128)(2,1)} %bitcast.193, bf16[1,7168,1024]{2,1,0:T(8,128)(2,1)} %refs_2_.7, bf16[1,7168,1024]{2,1,0:T(8,128)(2,1)} %refs_3_.7), custom_call_target="tpu_custom_call" | custom-call | flops 15032385536 | bytes 36700160 | tf_op jit(solution)/shard_map/pallas_call | solution.py:139
  185.4 3.2 add_convert_fusion.3
  191.1 14.7 %shard_map.67 = (bf16[2,256,3584]{2,1,0:T(8,128)(2,1)S(1)}, bf16[2,256,3584]{2,1,0:T(8,128)(2,1)}) custom-call(s32[2]{0:T(128)S(1)} %pad_add_fusion.place, bf16[512,1024]{1,0:T(8,128)(2,1)S(1)} %shard_map.66.hidden, bf16[1,1024,7168]{2,1,0:T(8,128)(2,1)} %wd.7, f32[512,1]{1,0:T(8,128)S(1)} %reshape.236.scale), custom_call_target="tpu_custom_call" | custom-call | flops 7516192768 | bytes 22020096 | tf_op jit(solution)/shard_map/pallas_call | solution.py:159
  211.9 11.1 %collective-permute-done.6 = bf16[4,2,32,1792]{3,2,0,1:T(8,128)(2,1)} collective-permute-done((bf16[4,2,32,1792]{3,2,0,1:T(8,128)(2,1)}, bf16[4,2,32,1792]{3,2,0,1:T(8,128)(2,1)}, u32[]{:S(2)}, u32[]{:S(2)}) %collective-permute-start.6) | collective-permute-done | bytes 917536 | tf_op jit(solution)/shard_map/ppermute | solution.py:32
  224.9 8.2 %collective-permute-done.8 = bf16[2,4,32,1792]{3,2,1,0:T(8,128)(2,1)} collective-permute-done((bf16[2,4,32,1792]{3,2,1,0:T(8,128)(2,1)}, bf16[2,4,32,1792]{3,2,1,0:T(8,128)(2,1)}, u32[]{:S(2)}, u32[]{:S(2)}) %collective-permute-start.8) | collective-permute-done | bytes 917536 | tf_op jit(solution)/shard_map/ppermute | solution.py:32
  235.1 7.7 %collective-permute-done.7 = bf16[4,32,1792]{2,1,0:T(8,128)(2,1)S(1)} collective-permute-done((bf16[4,32,1792]{2,1,0:T(8,128)(2,1)S(1)}, bf16[4,32,1792]{2,1,0:T(8,128)(2,1)S(1)}, u32[]{:S(2)}, u32[]{:S(2)}) %collective-permute-start.7) | collective-permute-done | bytes 458784 | tf_op jit(solution)/shard_map/ppermute | solution.py:32
  242.9 2.5 collective-permute-done.9
  249.2 3.2 add_convert_fusion.2
  254.4 8.6 %collective-permute-done.11 = bf16[32,3584]{1,0:T(8,128)(2,1)S(1)} collective-permute-done((bf16[32,3584]{1,0:T(8,128)(2,1)S(1)}, bf16[32,3584]{1,0:T(8,128)(2,1)S(1)}, u32[]{:S(2)}, u32[]{:S(2)}) %collective-permute-start.11) | collective-permute-done | bytes 229408 | tf_op jit(solution)/shard_map/ppermute | solution.py:32
  263.0 4.9 %collective-permute-done.12 = bf16[32,3584]{1,0:T(8,128)(2,1)S(1)} collective-permute-done((bf16[32,3584]{1,0:T(8,128)(2,1)S(1)}, bf16[32,3584]{1,0:T(8,128)(2,1)S(1)}, u32[]{:S(2)}, u32[]{:S(2)}) %collective-permute-start.12) | collective-permute-done | bytes 229408 | tf_op jit(solution)/shard_map/ppermute | solution.py:32
  268.0 4.8 %collective-permute-done.14 = bf16[4,2,32,1792]{3,2,0,1:T(8,128)(2,1)S(1)} collective-permute-done((bf16[4,2,32,1792]{3,2,0,1:T(8,128)(2,1)S(1)}, bf16[4,2,32,1792]{3,2,0,1:T(8,128)(2,1)S(1)}, u32[]{:S(2)}, u32[]{:S(2)}) %collective-permute-start.14) | collective-permute-done | bytes 917536 | tf_op jit(solution)/shard_map/ppermute | solution.py:32
  273.3 25.9 %shard_map.68.hidden = bf16[512,1024]{1,0:T(8,128)(2,1)S(1)} custom-call(s32[2]{0:T(128)S(1)} %pad_add_fusion.place, bf16[4,2,2,2,64,3584]{5,4,3,2,1,0:T(8,128)(2,1)} %bitcast.186, bf16[4,2,2,2,64,3584]{5,4,3,2,1,0:T(8,128)(2,1)} %bitcast.187, bf16[1,7168,1024]{2,1,0:T(8,128)(2,1)} %refs_2_.7, bf16[1,7168,1024]{2,1,0:T(8,128)(2,1)} %refs_3_.7), custom_call_target="tpu_custom_call" | custom-call | flops 15032385536 | bytes 36700160 | tf_op jit(solution)/shard_map/pallas_call | solution.py:139
  299.2 14.7 %shard_map.69 = (bf16[2,256,3584]{2,1,0:T(8,128)(2,1)S(1)}, bf16[2,256,3584]{2,1,0:T(8,128)(2,1)}) custom-call(s32[2]{0:T(128)S(1)} %pad_add_fusion.place, bf16[512,1024]{1,0:T(8,128)(2,1)S(1)} %shard_map.68.hidden, bf16[1,1024,7168]{2,1,0:T(8,128)(2,1)} %wd.7, f32[512,1]{1,0:T(8,128)S(1)} %reshape.237.scale), custom_call_target="tpu_custom_call" | custom-call | flops 7516192768 | bytes 22020096 | tf_op jit(solution)/shard_map/pallas_call | solution.py:159
  313.9 4.2 collective-permute-start.21
  319.6 10.5 %collective-permute-done.15 = bf16[4,32,1792]{2,1,0:T(8,128)(2,1)S(1)} collective-permute-done((bf16[4,32,1792]{2,1,0:T(8,128)(2,1)S(1)}, bf16[4,32,1792]{2,1,0:T(8,128)(2,1)S(1)}, u32[]{:S(2)}, u32[]{:S(2)}) %collective-permute-start.15) | collective-permute-done | bytes 458784 | tf_op jit(solution)/shard_map/ppermute | solution.py:32
  331.7 2.3 collective-permute-start.20
  334.0 25.9 %shard_map.70.hidden = bf16[512,1024]{1,0:T(8,128)(2,1)S(1)} custom-call(s32[2]{0:T(128)S(1)} %pad_add_fusion.place, bf16[4,2,2,2,64,3584]{5,4,3,2,1,0:T(8,128)(2,1)} %bitcast.188, bf16[4,2,2,2,64,3584]{5,4,3,2,1,0:T(8,128)(2,1)} %bitcast.189, bf16[1,7168,1024]{2,1,0:T(8,128)(2,1)} %refs_2_.7, bf16[1,7168,1024]{2,1,0:T(8,128)(2,1)} %refs_3_.7), custom_call_target="tpu_custom_call" | custom-call | flops 15032385536 | bytes 36700160 | tf_op jit(solution)/shard_map/pallas_call | solution.py:139
  361.0 14.7 %shard_map.71 = (bf16[2,256,3584]{2,1,0:T(8,128)(2,1)S(1)}, bf16[2,256,3584]{2,1,0:T(8,128)(2,1)}) custom-call(s32[2]{0:T(128)S(1)} %pad_add_fusion.place, bf16[512,1024]{1,0:T(8,128)(2,1)S(1)} %shard_map.70.hidden, bf16[1,1024,7168]{2,1,0:T(8,128)(2,1)} %wd.7, f32[512,1]{1,0:T(8,128)S(1)} %reshape.238.scale), custom_call_target="tpu_custom_call" | custom-call | flops 7516192768 | bytes 22020096 | tf_op jit(solution)/shard_map/pallas_call | solution.py:159
  379.4 20.5 %collective-permute-done.22 = bf16[4,2,32,1792]{3,2,0,1:T(8,128)(2,1)S(1)} collective-permute-done((bf16[4,2,32,1792]{3,2,0,1:T(8,128)(2,1)S(1)}, bf16[4,2,32,1792]{3,2,0,1:T(8,128)(2,1)S(1)}, u32[]{:S(2)}, u32[]{:S(2)}) %collective-permute-start.22) | collective-permute-done | bytes 917536 | tf_op jit(solution)/shard_map/ppermute | solution.py:32
  401.7 9.7 %collective-permute-done.23 = bf16[4,32,1792]{2,1,0:T(8,128)(2,1)S(1)} collective-permute-done((bf16[4,32,1792]{2,1,0:T(8,128)(2,1)S(1)}, bf16[4,32,1792]{2,1,0:T(8,128)(2,1)S(1)}, u32[]{:S(2)}, u32[]{:S(2)}) %collective-permute-start.23) | collective-permute-done | bytes 458784 | tf_op jit(solution)/shard_map/ppermute | solution.py:32
  415.8 2.3 collective-permute-start.28
  419.4 14.3 %collective-permute-done.32 = bf16[2,4,32,1792]{3,2,1,0:T(8,128)(2,1)S(1)} collective-permute-done((bf16[2,4,32,1792]{3,2,1,0:T(8,128)(2,1)S(1)}, bf16[2,4,32,1792]{3,2,1,0:T(8,128)(2,1)S(1)}, u32[]{:S(2)}, u32[]{:S(2)}) %collective-permute-start.32) | collective-permute-done | bytes 917536 | tf_op jit(solution)/shard_map/ppermute | solution.py:32
  434.3 2.9 collective-permute-done.30
  438.6 8.4 %collective-permute-done.33 = bf16[4,32,1792]{2,1,0:T(8,128)(2,1)S(1)} collective-permute-done((bf16[4,32,1792]{2,1,0:T(8,128)(2,1)S(1)}, bf16[4,32,1792]{2,1,0:T(8,128)(2,1)S(1)}, u32[]{:S(2)}, u32[]{:S(2)}) %collective-permute-start.33) | collective-permute-done | bytes 458784 | tf_op jit(solution)/shard_map/ppermute | solution.py:32
  452.5 5.4 %collective-permute-done.35 = bf16[32,3584]{1,0:T(8,128)(2,1)S(1)} collective-permute-done((bf16[32,3584]{1,0:T(8,128)(2,1)S(1)}, bf16[32,3584]{1,0:T(8,128)(2,1)S(1)}, u32[]{:S(2)}, u32[]{:S(2)}) %collective-permute-start.35) | collective-permute-done | bytes 229408 | tf_op jit(solution)/shard_map/ppermute | solution.py:32
  457.9 9.6 %collective-permute-done.36 = bf16[32,3584]{1,0:T(8,128)(2,1)S(1)} collective-permute-done((bf16[32,3584]{1,0:T(8,128)(2,1)S(1)}, bf16[32,3584]{1,0:T(8,128)(2,1)S(1)}, u32[]{:S(2)}, u32[]{:S(2)}) %collective-permute-start.36) | collective-permute-done | bytes 229408 | tf_op jit(solution)/shard_map/ppermute | solution.py:32
  (149 shorter events, 55.8 us)
Async XLA Ops:
  6.5 109.4 %all-gather.5.cloned.1.call-start = ((), (), s32[]{:S(2)}) async-start(), calls=%async_computation | async-start | bytes 15138816 | tf_op jit(solution)/shard_map/all_gather | solution.py:206
  8.7 264.6 %all-gather.7.cloned.1.call-start = ((), (), s32[]{:S(2)}) async-start(), calls=%async_computation.1 | async-start | bytes 15138816 | tf_op jit(solution)/shard_map/all_gather | solution.py:206
  158.4 26.9 %collective-permute-start.5 = (bf16[2,256,3584]{2,1,0:T(8,128)(2,1)}, bf16[2,256,3584]{2,1,0:T(8,128)(2,1)}, u32[]{:S(2)}, u32[]{:S(2)}) collective-permute-start(bf16[2,256,3584]{2,1,0:T(8,128)(2,1)} %get-tuple-element.19), channel_id=1, source_target_pairs={{0,1},{1,0},{2,3},{3,2},{4,5},{5,4},{6,7},{7,6},{8,9},{9,8},{10,11... | collective-permute-start | bytes 11010056 | tf_op jit(solution)/shard_map/ppermute | solution.py:32
  190.0 33.0 %collective-permute-start.6 = (bf16[4,2,32,1792]{3,2,0,1:T(8,128)(2,1)}, bf16[4,2,32,1792]{3,2,0,1:T(8,128)(2,1)}, u32[]{:S(2)}, u32[]{:S(2)}) collective-permute-start(bf16[4,2,32,1792]{3,2,0,1:T(8,128)(2,1)} %bitcast.185), channel_id=1, source_target_pairs={{0,4},{4,0},{1,5},{5,1},{2,6},{6,2},{3,7},{7,3},{8,12},{12,8},{9,1... | collective-permute-start | bytes 2752520 | tf_op jit(solution)/shard_map/ppermute | solution.py:32
  207.7 41.6 %collective-permute-start.13 = (bf16[2,256,3584]{2,1,0:T(8,128)(2,1)}, bf16[2,256,3584]{2,1,0:T(8,128)(2,1)}, u32[]{:S(2)}, u32[]{:S(2)}) collective-permute-start(bf16[2,256,3584]{2,1,0:T(8,128)(2,1)} %get-tuple-element.23), channel_id=1, source_target_pairs={{0,1},{1,0},{2,3},{3,2},{4,5},{5,4},{6,7},{7,6},{8,9},{9,8},{10,11... | collective-permute-start | bytes 11010056 | tf_op jit(solution)/shard_map/ppermute | solution.py:32
  210.9 22.2 %collective-permute-start.8 = (bf16[2,4,32,1792]{3,2,1,0:T(8,128)(2,1)}, bf16[2,4,32,1792]{3,2,1,0:T(8,128)(2,1)}, u32[]{:S(2)}, u32[]{:S(2)}) collective-permute-start(bf16[2,4,32,1792]{3,2,1,0:T(8,128)(2,1)} %dynamic-slice_bitcast_fusion.3), channel_id=1, source_target_pairs={{0,2},{1,3},{2,0},{3,1},{4,6},{5,7},{6,4},{7,5},{8,10},{9,11},{10,... | collective-permute-start | bytes 2752520 | tf_op jit(solution)/shard_map/ppermute | solution.py:32
  224.5 18.3 %collective-permute-start.7 = (bf16[4,32,1792]{2,1,0:T(8,128)(2,1)S(1)}, bf16[4,32,1792]{2,1,0:T(8,128)(2,1)S(1)}, u32[]{:S(2)}, u32[]{:S(2)}) collective-permute-start(bf16[4,32,1792]{2,1,0:T(8,128)(2,1)S(1)} %dynamic-slice_bitcast_fusion.7), channel_id=1, source_target_pairs={{0,2},{1,3},{2,0},{3,1},{4,6},{5,7},{6,4},{7,5},{8,10},{9,11},{10,... | collective-permute-start | bytes 1376264 | tf_op jit(solution)/shard_map/ppermute | solution.py:32
  234.6 10.8 %collective-permute-start.9 = (bf16[4,32,1792]{2,1,0:T(8,128)(2,1)S(1)}, bf16[4,32,1792]{2,1,0:T(8,128)(2,1)S(1)}, u32[]{:S(2)}, u32[]{:S(2)}) collective-permute-start(bf16[4,32,1792]{2,1,0:T(8,128)(2,1)S(1)} %slice_bitcast_fusion.6), channel_id=1, source_target_pairs={{0,4},{4,0},{1,5},{5,1},{2,6},{6,2},{3,7},{7,3},{8,12},{12,8},{9,1... | collective-permute-start | bytes 1376264 | tf_op jit(solution)/shard_map/ppermute | solution.py:32
  246.1 16.9 %collective-permute-start.11 = (bf16[32,3584]{1,0:T(8,128)(2,1)S(1)}, bf16[32,3584]{1,0:T(8,128)(2,1)S(1)}, u32[]{:S(2)}, u32[]{:S(2)}) collective-permute-start(bf16[32,3584]{1,0:T(8,128)(2,1)S(1)} %get-tuple-element.49), channel_id=1, source_target_pairs={{0,16},{8,24},{16,0},{24,8},{1,17},{9,25},{17,1},{25,9},{2,18},{10... | collective-permute-start | bytes 688136 | tf_op jit(solution)/shard_map/ppermute | solution.py:32
  247.9 20.0 %collective-permute-start.12 = (bf16[32,3584]{1,0:T(8,128)(2,1)S(1)}, bf16[32,3584]{1,0:T(8,128)(2,1)S(1)}, u32[]{:S(2)}, u32[]{:S(2)}) collective-permute-start(bf16[32,3584]{1,0:T(8,128)(2,1)S(1)} %get-tuple-element.50), channel_id=1, source_target_pairs={{0,8},{8,16},{16,24},{24,0},{1,9},{9,17},{17,25},{25,1},{2,10},{10... | collective-permute-start | bytes 688136 | tf_op jit(solution)/shard_map/ppermute | solution.py:32
  252.8 20.2 %collective-permute-start.16 = (bf16[2,4,32,1792]{3,2,1,0:T(8,128)(2,1)S(1)}, bf16[2,4,32,1792]{3,2,1,0:T(8,128)(2,1)S(1)}, u32[]{:S(2)}, u32[]{:S(2)}) collective-permute-start(bf16[2,4,32,1792]{3,2,1,0:T(8,128)(2,1)S(1)} %dynamic-slice_bitcast_fusion.2), channel_id=1, source_target_pairs={{0,2},{1,3},{2,0},{3,1},{4,6},{5,7},{6,4},{7,5},{8,10},{9,11},{10,... | collective-permute-start | bytes 2752520 | tf_op jit(solution)/shard_map/ppermute | solution.py:32
  254.1 18.7 %collective-permute-start.14 = (bf16[4,2,32,1792]{3,2,0,1:T(8,128)(2,1)S(1)}, bf16[4,2,32,1792]{3,2,0,1:T(8,128)(2,1)S(1)}, u32[]{:S(2)}, u32[]{:S(2)}) collective-permute-start(bf16[4,2,32,1792]{3,2,0,1:T(8,128)(2,1)S(1)} %bitcast.202), channel_id=1, source_target_pairs={{0,4},{4,0},{1,5},{5,1},{2,6},{6,2},{3,7},{7,3},{8,12},{12,8},{9,1... | collective-permute-start | bytes 2752520 | tf_op jit(solution)/shard_map/ppermute | solution.py:32
  313.9 46.2 %collective-permute-start.21 = (bf16[2,256,3584]{2,1,0:T(8,128)(2,1)}, bf16[2,256,3584]{2,1,0:T(8,128)(2,1)S(1)}, u32[]{:S(2)}, u32[]{:S(2)}) collective-permute-start(bf16[2,256,3584]{2,1,0:T(8,128)(2,1)} %get-tuple-element.26), channel_id=1, source_target_pairs={{0,1},{1,0},{2,3},{3,2},{4,5},{5,4},{6,7},{7,6},{8,9},{9,8},{10,11... | collective-permute-start | bytes 11010056 | tf_op jit(solution)/shard_map/ppermute | solution.py:32
  318.0 12.1 %collective-permute-start.15 = (bf16[4,32,1792]{2,1,0:T(8,128)(2,1)S(1)}, bf16[4,32,1792]{2,1,0:T(8,128)(2,1)S(1)}, u32[]{:S(2)}, u32[]{:S(2)}) collective-permute-start(bf16[4,32,1792]{2,1,0:T(8,128)(2,1)S(1)} %dynamic-slice_bitcast_fusion.6), channel_id=1, source_target_pairs={{0,2},{1,3},{2,0},{3,1},{4,6},{5,7},{6,4},{7,5},{8,10},{9,11},{10,... | collective-permute-start | bytes 1376264 | tf_op jit(solution)/shard_map/ppermute | solution.py:32
  318.4 11.9 %collective-permute-start.17 = (bf16[4,32,1792]{2,1,0:T(8,128)(2,1)S(1)}, bf16[4,32,1792]{2,1,0:T(8,128)(2,1)S(1)}, u32[]{:S(2)}, u32[]{:S(2)}) collective-permute-start(bf16[4,32,1792]{2,1,0:T(8,128)(2,1)S(1)} %slice_bitcast_fusion.4), channel_id=1, source_target_pairs={{0,4},{4,0},{1,5},{5,1},{2,6},{6,2},{3,7},{7,3},{8,12},{12,8},{9,1... | collective-permute-start | bytes 1376264 | tf_op jit(solution)/shard_map/ppermute | solution.py:32
  330.4 29.4 %collective-permute-start.18 = (bf16[32,3584]{1,0:T(8,128)(2,1)S(1)}, bf16[32,3584]{1,0:T(8,128)(2,1)S(1)}, u32[]{:S(2)}, u32[]{:S(2)}) collective-permute-start(bf16[32,3584]{1,0:T(8,128)(2,1)S(1)} %get-tuple-element.45), channel_id=1, source_target_pairs={{0,24},{8,0},{16,8},{24,16},{1,25},{9,1},{17,9},{25,17},{2,26},{10... | collective-permute-start | bytes 688136 | tf_op jit(solution)/shard_map/ppermute | solution.py:32
  330.6 29.3 %collective-permute-start.19 = (bf16[32,3584]{1,0:T(8,128)(2,1)S(1)}, bf16[32,3584]{1,0:T(8,128)(2,1)S(1)}, u32[]{:S(2)}, u32[]{:S(2)}) collective-permute-start(bf16[32,3584]{1,0:T(8,128)(2,1)S(1)} %get-tuple-element.46), channel_id=1, source_target_pairs={{0,16},{8,24},{16,0},{24,8},{1,17},{9,25},{17,1},{25,9},{2,18},{10... | collective-permute-start | bytes 688136 | tf_op jit(solution)/shard_map/ppermute | solution.py:32
  331.7 28.2 %collective-permute-start.20 = (bf16[32,3584]{1,0:T(8,128)(2,1)S(1)}, bf16[32,3584]{1,0:T(8,128)(2,1)S(1)}, u32[]{:S(2)}, u32[]{:S(2)}) collective-permute-start(bf16[32,3584]{1,0:T(8,128)(2,1)S(1)} %get-tuple-element.47), channel_id=1, source_target_pairs={{0,8},{8,16},{16,24},{24,0},{1,9},{9,17},{17,25},{25,1},{2,10},{10... | collective-permute-start | bytes 688136 | tf_op jit(solution)/shard_map/ppermute | solution.py:32
  375.7 36.8 %collective-permute-start.29 = (bf16[2,256,3584]{2,1,0:T(8,128)(2,1)}, bf16[2,256,3584]{2,1,0:T(8,128)(2,1)S(1)}, u32[]{:S(2)}, u32[]{:S(2)}) collective-permute-start(bf16[2,256,3584]{2,1,0:T(8,128)(2,1)} %get-tuple-element.30), channel_id=1, source_target_pairs={{0,1},{1,0},{2,3},{3,2},{4,5},{5,4},{6,7},{7,6},{8,9},{9,8},{10,11... | collective-permute-start | bytes 11010056 | tf_op jit(solution)/shard_map/ppermute | solution.py:32
  377.9 22.0 %collective-permute-start.22 = (bf16[4,2,32,1792]{3,2,0,1:T(8,128)(2,1)S(1)}, bf16[4,2,32,1792]{3,2,0,1:T(8,128)(2,1)S(1)}, u32[]{:S(2)}, u32[]{:S(2)}) collective-permute-start(bf16[4,2,32,1792]{3,2,0,1:T(8,128)(2,1)S(1)} %bitcast.204), channel_id=1, source_target_pairs={{0,4},{4,0},{1,5},{5,1},{2,6},{6,2},{3,7},{7,3},{8,12},{12,8},{9,1... | collective-permute-start | bytes 2752520 | tf_op jit(solution)/shard_map/ppermute | solution.py:32
  379.1 22.0 %collective-permute-start.24 = (bf16[2,4,32,1792]{3,2,1,0:T(8,128)(2,1)S(1)}, bf16[2,4,32,1792]{3,2,1,0:T(8,128)(2,1)S(1)}, u32[]{:S(2)}, u32[]{:S(2)}) collective-permute-start(bf16[2,4,32,1792]{3,2,1,0:T(8,128)(2,1)S(1)} %dynamic-slice_bitcast_fusion.1), channel_id=1, source_target_pairs={{0,2},{1,3},{2,0},{3,1},{4,6},{5,7},{6,4},{7,5},{8,10},{9,11},{10,... | collective-permute-start | bytes 2752520 | tf_op jit(solution)/shard_map/ppermute | solution.py:32
  400.1 11.3 %collective-permute-start.23 = (bf16[4,32,1792]{2,1,0:T(8,128)(2,1)S(1)}, bf16[4,32,1792]{2,1,0:T(8,128)(2,1)S(1)}, u32[]{:S(2)}, u32[]{:S(2)}) collective-permute-start(bf16[4,32,1792]{2,1,0:T(8,128)(2,1)S(1)} %dynamic-slice_bitcast_fusion.5), channel_id=1, source_target_pairs={{0,2},{1,3},{2,0},{3,1},{4,6},{5,7},{6,4},{7,5},{8,10},{9,11},{10,... | collective-permute-start | bytes 1376264 | tf_op jit(solution)/shard_map/ppermute | solution.py:32
  401.4 11.0 %collective-permute-start.25 = (bf16[4,32,1792]{2,1,0:T(8,128)(2,1)S(1)}, bf16[4,32,1792]{2,1,0:T(8,128)(2,1)S(1)}, u32[]{:S(2)}, u32[]{:S(2)}) collective-permute-start(bf16[4,32,1792]{2,1,0:T(8,128)(2,1)S(1)} %slice_bitcast_fusion.2), channel_id=1, source_target_pairs={{0,4},{4,0},{1,5},{5,1},{2,6},{6,2},{3,7},{7,3},{8,12},{12,8},{9,1... | collective-permute-start | bytes 1376264 | tf_op jit(solution)/shard_map/ppermute | solution.py:32
  413.7 20.0 %collective-permute-start.32 = (bf16[2,4,32,1792]{3,2,1,0:T(8,128)(2,1)S(1)}, bf16[2,4,32,1792]{3,2,1,0:T(8,128)(2,1)S(1)}, u32[]{:S(2)}, u32[]{:S(2)}) collective-permute-start(bf16[2,4,32,1792]{3,2,1,0:T(8,128)(2,1)S(1)} %dynamic-slice_bitcast_fusion), channel_id=1, source_target_pairs={{0,2},{1,3},{2,0},{3,1},{4,6},{5,7},{6,4},{7,5},{8,10},{9,11},{10,... | collective-permute-start | bytes 2752520 | tf_op jit(solution)/shard_map/ppermute | solution.py:32
  414.4 34.4 %collective-permute-start.26 = (bf16[32,3584]{1,0:T(8,128)(2,1)S(1)}, bf16[32,3584]{1,0:T(8,128)(2,1)S(1)}, u32[]{:S(2)}, u32[]{:S(2)}) collective-permute-start(bf16[32,3584]{1,0:T(8,128)(2,1)S(1)} %get-tuple-element.39), channel_id=1, source_target_pairs={{0,24},{8,0},{16,8},{24,16},{1,25},{9,1},{17,9},{25,17},{2,26},{10... | collective-permute-start | bytes 688136 | tf_op jit(solution)/shard_map/ppermute | solution.py:32
  414.5 36.4 %collective-permute-start.27 = (bf16[32,3584]{1,0:T(8,128)(2,1)S(1)}, bf16[32,3584]{1,0:T(8,128)(2,1)S(1)}, u32[]{:S(2)}, u32[]{:S(2)}) collective-permute-start(bf16[32,3584]{1,0:T(8,128)(2,1)S(1)} %get-tuple-element.40), channel_id=1, source_target_pairs={{0,16},{8,24},{16,0},{24,8},{1,17},{9,25},{17,1},{25,9},{2,18},{10... | collective-permute-start | bytes 688136 | tf_op jit(solution)/shard_map/ppermute | solution.py:32
  415.8 35.0 %collective-permute-start.28 = (bf16[32,3584]{1,0:T(8,128)(2,1)S(1)}, bf16[32,3584]{1,0:T(8,128)(2,1)S(1)}, u32[]{:S(2)}, u32[]{:S(2)}) collective-permute-start(bf16[32,3584]{1,0:T(8,128)(2,1)S(1)} %get-tuple-element.41), channel_id=1, source_target_pairs={{0,8},{8,16},{16,24},{24,0},{1,9},{9,17},{17,25},{25,1},{2,10},{10... | collective-permute-start | bytes 688136 | tf_op jit(solution)/shard_map/ppermute | solution.py:32
  418.3 18.9 %collective-permute-start.30 = (bf16[4,2,32,1792]{3,2,0,1:T(8,128)(2,1)S(1)}, bf16[4,2,32,1792]{3,2,0,1:T(8,128)(2,1)S(1)}, u32[]{:S(2)}, u32[]{:S(2)}) collective-permute-start(bf16[4,2,32,1792]{3,2,0,1:T(8,128)(2,1)S(1)} %bitcast.203), channel_id=1, source_target_pairs={{0,4},{4,0},{1,5},{5,1},{2,6},{6,2},{3,7},{7,3},{8,12},{12,8},{9,1... | collective-permute-start | bytes 2752520 | tf_op jit(solution)/shard_map/ppermute | solution.py:32
  434.0 13.0 %collective-permute-start.33 = (bf16[4,32,1792]{2,1,0:T(8,128)(2,1)S(1)}, bf16[4,32,1792]{2,1,0:T(8,128)(2,1)S(1)}, u32[]{:S(2)}, u32[]{:S(2)}) collective-permute-start(bf16[4,32,1792]{2,1,0:T(8,128)(2,1)S(1)} %slice_bitcast_fusion), channel_id=1, source_target_pairs={{0,4},{4,0},{1,5},{5,1},{2,6},{6,2},{3,7},{7,3},{8,12},{12,8},{9,1... | collective-permute-start | bytes 1376264 | tf_op jit(solution)/shard_map/ppermute | solution.py:32
  437.4 9.7 %collective-permute-start.31 = (bf16[4,32,1792]{2,1,0:T(8,128)(2,1)S(1)}, bf16[4,32,1792]{2,1,0:T(8,128)(2,1)S(1)}, u32[]{:S(2)}, u32[]{:S(2)}) collective-permute-start(bf16[4,32,1792]{2,1,0:T(8,128)(2,1)S(1)} %dynamic-slice_bitcast_fusion.4), channel_id=1, source_target_pairs={{0,2},{1,3},{2,0},{3,1},{4,6},{5,7},{6,4},{7,5},{8,10},{9,11},{10,... | collective-permute-start | bytes 1376264 | tf_op jit(solution)/shard_map/ppermute | solution.py:32
  447.4 10.5 %collective-permute-start.35 = (bf16[32,3584]{1,0:T(8,128)(2,1)S(1)}, bf16[32,3584]{1,0:T(8,128)(2,1)S(1)}, u32[]{:S(2)}, u32[]{:S(2)}) collective-permute-start(bf16[32,3584]{1,0:T(8,128)(2,1)S(1)} %get-tuple-element.43), channel_id=1, source_target_pairs={{0,16},{8,24},{16,0},{24,8},{1,17},{9,25},{17,1},{25,9},{2,18},{10... | collective-permute-start | bytes 688136 | tf_op jit(solution)/shard_map/ppermute | solution.py:32
  448.8 18.6 %collective-permute-start.36 = (bf16[32,3584]{1,0:T(8,128)(2,1)S(1)}, bf16[32,3584]{1,0:T(8,128)(2,1)S(1)}, u32[]{:S(2)}, u32[]{:S(2)}) collective-permute-start(bf16[32,3584]{1,0:T(8,128)(2,1)S(1)} %get-tuple-element.44), channel_id=1, source_target_pairs={{0,8},{8,16},{16,24},{24,0},{1,9},{9,17},{17,25},{25,1},{2,10},{10... | collective-permute-start | bytes 688136 | tf_op jit(solution)/shard_map/ppermute | solution.py:32
  (12 other events, 103.6 us)
Sparse Core Ops, SparseCore 0:
  10.2 105.6 all-gather.4
  118.8 113.4 all-gather.6

commit v2 on v1

--- a/solution.py
+++ b/solution.py
@@ -9,8 +9,8 @@
 
 
 route_scale = 2.827
-n_gathers = 2
 n_calls = 4
+n_walked = 2
 
 
 class Phase:
@@ -31,8 +31,8 @@
                 pairs.append((out * self.inner_n + low, to))
         return lax.ppermute(value, self.axis, pairs)
 
-    def gather(self, value):
-        return jnp.stack([value] + [self.shift(value, s) for s in range(1, self.n)])
+    def gather(self, value, axis=0):
+        return jnp.stack([value] + [self.shift(value, s) for s in range(1, self.n)], axis=axis)
 
     def ordered(self, value, axis):
         return jnp.take(value, (self.me - jnp.arange(self.n)) % self.n, axis=axis)
@@ -106,7 +106,7 @@
     rows = tok_rows // n_calls
     each = n_aa * n_high * rows
     tall = n_low * each
-    block = 896 if width % 896 == 0 else width
+    block = 1792 if width % 1792 == 0 else width
     per = width // block
     steps = n_ba * per
     place = jnp.stack([feat.me, pair.me]).astype(jnp.int32)
@@ -119,22 +119,29 @@
     scores = pair.gather(scores)
     own = jnp.arange(experts, dtype=jnp.int32)[:, None] == mine
     scores = jnp.sum(jnp.where(own, scores, 0.0), axis=3)
-    scores = wide.ordered(zed.ordered(scores, 2), 1)
-    scores = jnp.swapaxes(scores, 1, 2)
+    walked_scores = jnp.swapaxes(scores, 1, 2)
+    scores = wide.ordered(zed.ordered(walked_scores, 1), 2)
 
     def source(k, place):
         return (place[0] + n_ba - k // per) % n_ba
 
-    def hidden_of(gathered, number):
-        specs = [
-            pl.BlockSpec(
-                (n_aa, 1, n_high, 1, rows, block),
-                functools.partial(
-                    lambda s, k, place: (0, source(k, place), 0, (place[1] + n_low - s) % n_low, number, k % per), s
-                ),
-            )
-            for s in range(n_low)
-        ]
+    def hidden_of(arrays, number):
+        if len(arrays) == 1:
+            arrays = arrays * n_low
+            specs = [
+                pl.BlockSpec(
+                    (n_aa, 1, n_high, 1, rows, block),
+                    functools.partial(
+                        lambda s, k, place: (0, source(k, place), 0, (place[1] + n_low - s) % n_low, number, k % per),
+                        s,
+                    ),
+                )
+                for s in range(n_low)
+            ]
+        else:
+            specs = [
+                pl.BlockSpec((1, n_aa, n_high, rows, block), lambda k, place: (k // per, 0, 0, 0, k % per))
+            ] * n_low
         weights = pl.BlockSpec((1, block, hidden_n), lambda k, place: (0, source(k, place) * per + k % per, 0))
         return pl.pallas_call(
             functools.partial(hidden_body, steps),
@@ -151,11 +158,11 @@
                 transcendentals=tall * hidden_n,
                 bytes_accessed=4 * n_ba * width * hidden_n + 2 * tall * n_ba * width,
             ),
-            compiler_params=pltpu.CompilerParams(vmem_limit_bytes=48 * 1024 * 1024),
-        )(place, *[gathered] * n_low, w_gate, w_up)
+            compiler_params=pltpu.CompilerParams(vmem_limit_bytes=60 * 1024 * 1024),
+        )(place, *arrays, w_gate, w_up)
 
     def out_of(hidden, number):
-        scale = lax.slice_in_dim(scores, number * rows, (number + 1) * rows, axis=3).reshape(-1, 1)
+        scale = lax.slice_in_dim(walked_scores if number < n_walked else scores, number * rows, (number + 1) * rows, axis=3).reshape(-1, 1)
         return pl.pallas_call(
             down_body,
             grid_spec=pltpu.PrefetchScalarGridSpec(
@@ -174,61 +181,73 @@
                 transcendentals=0,
                 bytes_accessed=2 * n_ba * width * hidden_n + 2 * tall * n_ba * width,
             ),
-            compiler_params=pltpu.CompilerParams(vmem_limit_bytes=48 * 1024 * 1024),
+            compiler_params=pltpu.CompilerParams(vmem_limit_bytes=60 * 1024 * 1024),
         )(place, hidden, w_down, scale)
 
-    def give_back(outs):
+    def give_back(outs, moving):
         arrived = pair.send(outs)
         yield []
         value = total_of(outs[0], arrived).reshape(n_ba, n_aa, n_high, rows, width)
         middle = width // 256 * 128
         first, second = value[..., :middle], value[..., middle:]
         sides = feat.blocks(first, 0, False)
-        walls = wide.blocks(second, 2, True)
+        walls = wide.blocks(second, 2, moving)
         got_a, got_b = feat.send(sides), wide.send(walls)
         yield [value]
         first = total_of(sides[0], got_a)
         second = total_of(walls[0], got_b)
-        walls = wide.blocks(first, 1, True)
+        walls = wide.blocks(first, 1, moving)
         sides = feat.blocks(second, 0, False)
         got_a, got_b = wide.send(walls), feat.send(sides)
         yield [first, second]
         value = jnp.concatenate([total_of(walls[0], got_a), total_of(sides[0], got_b)], axis=-1)
-        floors = zed.blocks(value, 0, True)
+        floors = zed.blocks(value, 0, moving)
         arrived = zed.send(floors)
         yield [value]
         yield [total_of(floors[0], arrived)]
 
-    each_gather = tok_rows // n_gathers
-    gathered = []
-    for c in range(n_gathers):
-        piece = lax.slice_in_dim(tokens, c * each_gather, (c + 1) * each_gather, axis=0)
-        piece = lax.all_gather(piece, ("aa", "ba", "col"), axis=0, tiled=False)
-        gathered.append(piece.reshape(n_aa, n_ba, n_high, n_low, each_gather, width))
+    def walk(piece):
+        value = zed.gather(piece)
+        middle = width // 256 * 128
+        first, second = value[..., :middle], value[..., middle:]
+        first = wide.gather(first, 1)
+        second = feat.gather(second)
+        first = feat.gather(first)
+        second = wide.gather(second, 2)
+        value = jnp.concatenate([first, second], axis=-1)
+        return [value] + [pair.shift(value, s) for s in range(1, n_low)]
+
+    begin = n_walked * rows
+    rest = lax.slice_in_dim(tokens, begin, tok_rows, axis=0)
+    rest = lax.all_gather(rest, ("aa", "ba", "col"), axis=0, tiled=False)
+    rest = [rest.reshape(n_aa, n_ba, n_high, n_low, tok_rows - begin, width)]
+    sources = [
+        walk(lax.slice_in_dim(tokens, c * rows, (c + 1) * rows, axis=0)) for c in range(n_walked)
+    ] + [rest] * (n_calls - n_walked)
 
     def tie(value, others):
         return lax.optimization_barrier((value, *others))[0] if others else value
 
-    per_gather = n_calls // n_gathers
     sums, last = [], {}
 
     def step(number):
         last[number] = next(sums[number])
         return last[number]
 
-    plan = [((), ()), ((), (0,)), ((1, 0, 1, 0, 1), ()), ((), (2, 0, 1))]
     outs = []
     for number in range(n_calls):
-        before, between = plan[number]
-        ready = [v for c in before for v in step(c)]
-        hidden = hidden_of(tie(gathered[number // per_gather], ready + outs), number % per_gather)
-        ready = [v for c in between for v in step(c)]
-        outs = list(out_of(tie(hidden, ready), number))
-        sums.append(give_back(outs))
+        before = step(number - 3) if number >= 3 else []
+        first, *others = sources[number]
+        first = tie(first, before + outs)
+        hidden = hidden_of([first] + others, max(number - n_walked, 0))
+        between = [v for back in (3, 2, 1) if number >= back for v in step(number - back)]
+        outs = list(out_of(tie(hidden, between), number))
+        sums.append(give_back(outs, number >= n_walked))
         step(number)
-    for number in range(n_calls):
-        for last[number] in sums[number]:
-            pass
+    for _ in range(5):
+        for number in range(n_calls):
+            for last[number] in sums[number]:
+                break
     return jnp.concatenate([last[c][0] for c in range(n_calls)], axis=0)
 
 

time: 482 us -> 531 us (1.10)
  waiting for transfers between devices: 226 us -> 254 us
  starting transfers between devices: 40.6 us -> 66.5 us
  Pallas kernels: 163 us -> 147 us
  other arithmetic: 17.6 us -> 29.2 us
    ppermute x37 -> x53, waiting for transfers between devices: 136 us -> 254 us  [shift(): return lax.ppermute(value, self.axis, pairs)]
    all_gather x2 -> x1, waiting for transfers between devices: 90 us -> 0.01 us  [on_device(): rest = lax.all_gather(rest, ('aa', 'ba', 'col'), axis=0, tiled=False)]
    ppermute x37 -> x53, starting transfers between devices: 40.5 us -> 66.5 us  [shift(): return lax.ppermute(value, self.axis, pairs)]
    pallas_call x4, Pallas kernels: 104 us -> 93.4 us  [hidden_of(): pl.pallas_call(functools.partial(hidden_body, steps), grid_spec=pltpu.Pre...]
    pallas_call x4, Pallas kernels: 58.8 us -> 53.4 us  [out_of(): pl.pallas_call(down_body, grid_spec=pltpu.PrefetchScalarGridSpec(num_scal...]
  transfers between devices with their start and end apart: 39 -> 54, of which waited for: 23 -> 33; matrix products, arithmetic and copies ran while one was open for 5% -> 8% of each run, Pallas kernels for 23% -> 28%
where the time goes in v2:
time: 531 us; the launch traced here: 526 us
  waiting for transfers between devices  254 us (48%)
  Pallas kernels  147 us (28%)
  starting transfers between devices  66.5 us (13%)
  other arithmetic  29.2 us (5%)
  local copies, waits for them, and re-layouts  15.2 us (3%)
  between operations  14.1 us (3%)
    ppermute x53, waiting for transfers between devices, shift(): return lax.ppermute(value, self.axis, pairs)  254 us
    pallas_call x4, Pallas kernels, hidden_of(): pl.pallas_call(functools.partial(hidden_body, steps), grid_spec=pltpu.Pre...  93.4 us
    ppermute x53, starting transfers between devices, shift(): return lax.ppermute(value, self.axis, pairs)  66.5 us
    pallas_call x4, Pallas kernels, out_of(): pl.pallas_call(down_body, grid_spec=pltpu.PrefetchScalarGridSpec(num_scal...  53.4 us
    convert_element_type x24, other arithmetic, total_of(): return total.astype(jnp.bfloat16)  18.6 us
  transfers between devices with their start and end apart: 54, of which 33 were waited for; matrix products, arithmetic and copies ran while one was open for 8% of the time, Pallas kernels for 28%

profile of v2, /device:TPU:11, one launch (start us, length us, event | category | flops | bytes accessed | tf_op | source)
XLA Modules:
  0.0 525.8 jit_solution(16778459793560586663)
XLA Ops:
  16.0 15.3 %collective-permute-done.1 = bf16[32,3584]{1,0:T(8,128)(2,1)S(1)} collective-permute-done((bf16[32,3584]{1,0:T(8,128)(2,1)S(1)}, bf16[32,3584]{1,0:T(8,128)(2,1)S(1)}, u32[]{:S(2)}, u32[]{:S(2)}) %collective-permute-start.1) | collective-permute-done | bytes 229408 | tf_op jit(solution)/shard_map/ppermute | solution.py:32
  31.4 9.7 %collective-permute-done = bf16[32,3584]{1,0:T(8,128)(2,1)S(1)} collective-permute-done((bf16[32,3584]{1,0:T(8,128)(2,1)S(1)}, bf16[32,3584]{1,0:T(8,128)(2,1)S(1)}, u32[]{:S(2)}, u32[]{:S(2)}) %collective-permute-start) | collective-permute-done | bytes 229408 | tf_op jit(solution)/shard_map/ppermute | solution.py:32
  42.9 10.9 %collective-permute-done.5 = bf16[4,32,1792]{2,1,0:T(8,128)(2,1)S(1)} collective-permute-done((bf16[4,32,1792]{2,1,0:T(8,128)(2,1)S(1)}, bf16[4,32,1792]{2,1,0:T(8,128)(2,1)S(1)}, u32[]{:S(2)}, u32[]{:S(2)}) %collective-permute-start.5) | collective-permute-done | bytes 458784 | tf_op jit(solution)/shard_map/ppermute | solution.py:32
  56.7 29.1 %collective-permute-done.6 = bf16[2,4,32,1792]{3,2,1,0:T(8,128)(2,1)S(1)} collective-permute-done((bf16[2,4,32,1792]{3,2,1,0:T(8,128)(2,1)S(1)}, bf16[2,4,32,1792]{3,2,1,0:T(8,128)(2,1)S(1)}, u32[]{:S(2)}, u32[]{:S(2)}) %collective-permute-start.6) | collective-permute-done | bytes 917536 | tf_op jit(solution)/shard_map/ppermute | solution.py:32
  93.8 18.4 %collective-permute-done.23 = bf16[32,3584]{1,0:T(8,128)(2,1)S(1)} collective-permute-done((bf16[32,3584]{1,0:T(8,128)(2,1)S(1)}, bf16[32,3584]{1,0:T(8,128)(2,1)S(1)}, u32[]{:S(2)}, u32[]{:S(2)}) %collective-permute-start.23) | collective-permute-done | bytes 229408 | tf_op jit(solution)/shard_map/ppermute | solution.py:32
  114.6 18.1 %collective-permute-done.21 = bf16[32,3584]{1,0:T(8,128)(2,1)S(1)} collective-permute-done((bf16[32,3584]{1,0:T(8,128)(2,1)S(1)}, bf16[32,3584]{1,0:T(8,128)(2,1)S(1)}, u32[]{:S(2)}, u32[]{:S(2)}) %collective-permute-start.21) | collective-permute-done | bytes 229408 | tf_op jit(solution)/shard_map/ppermute | solution.py:32
  134.1 9.5 %collective-permute-done.26 = bf16[4,32,1792]{2,1,0:T(8,128)(2,1)S(1)} collective-permute-done((bf16[4,32,1792]{2,1,0:T(8,128)(2,1)S(1)}, bf16[4,32,1792]{2,1,0:T(8,128)(2,1)S(1)}, u32[]{:S(2)}, u32[]{:S(2)}) %collective-permute-start.26) | collective-permute-done | bytes 458784 | tf_op jit(solution)/shard_map/ppermute | solution.py:32
  147.5 6.6 %collective-permute-start.10 = (f32[16,128]{1,0:T(8,128)S(1)}, f32[16,128]{1,0:T(8,128)S(1)}, u32[]{:S(2)}, u32[]{:S(2)}) collective-permute-start(f32[16,128]{1,0:T(8,128)S(1)} %select_reduce_fusion), channel_id=1, source_target_pairs={{0,24},{8,0},{16,8},{24,16},{1,25},{9,1},{17,9},{25,17},{2,26},{10... | collective-permute-start | bytes 24584 | tf_op jit(solution)/shard_map/ppermute | solution.py:32
  160.2 5.0 collective-permute-done.11
  173.8 23.2 %shard_map.64.hidden = bf16[512,1024]{1,0:T(8,128)(2,1)} custom-call(s32[2]{0:T(128)} %pad_add_fusion.place, bf16[2,4,2,32,3584]{4,3,2,1,0:T(8,128)(2,1)} %maximum_maximum_fusion.refs_0_, bf16[2,4,2,32,3584]{4,3,2,1,0:T(8,128)(2,1)} %collective-permute-done.7.refs_1_, bf16[1,7168,1024]{2,1,0:T(8,128)(2,1)} %refs_2_.7, bf16[1,7168,1024]{2,1,0:T(8,128)(2,1)} %refs_3_.7), custom_call_target="tpu_custom_call" | custom-call | flops 15032385536 | bytes 36700160 | tf_op jit(solution)/shard_map/pallas_call | solution.py:146
  197.1 13.4 %shard_map.65 = (bf16[2,256,3584]{2,1,0:T(8,128)(2,1)}, bf16[2,256,3584]{2,1,0:T(8,128)(2,1)}) custom-call(s32[2]{0:T(128)} %pad_add_fusion.place, bf16[512,1024]{1,0:T(8,128)(2,1)} %shard_map.64.hidden, bf16[1,1024,7168]{2,1,0:T(8,128)(2,1)} %wd.7, f32[512,1]{1,0:T(8,128)} %reshape.229.scale), custom_call_target="tpu_custom_call" | custom-call | flops 7516192768 | bytes 22020096 | tf_op jit(solution)/shard_map/pallas_call | solution.py:166
  215.0 23.2 %shard_map.66.hidden = bf16[512,1024]{1,0:T(8,128)(2,1)} custom-call(s32[2]{0:T(128)} %pad_add_fusion.place, bf16[2,4,2,32,3584]{4,3,2,1,0:T(8,128)(2,1)} %maximum_maximum_fusion.1.refs_0_, bf16[2,4,2,32,3584]{4,3,2,1,0:T(8,128)(2,1)} %collective-permute-done.28.refs_1_, bf16[1,7168,1024]{2,1,0:T(8,128)(2,1)} %refs_2_.7, bf16[1,7168,1024]{2,1,0:T(8,128)(2,1)} %refs_3_.7), custom_call_target="tpu_custom_call" | custom-call | flops 15032385536 | bytes 36700160 | tf_op jit(solution)/shard_map/pallas_call | solution.py:146
  238.2 4.0 add_convert_fusion.3
  245.9 13.5 %shard_map.67 = (bf16[2,256,3584]{2,1,0:T(8,128)(2,1)}, bf16[2,256,3584]{2,1,0:T(8,128)(2,1)}) custom-call(s32[2]{0:T(128)} %pad_add_fusion.place, bf16[512,1024]{1,0:T(8,128)(2,1)} %shard_map.66.hidden, bf16[1,1024,7168]{2,1,0:T(8,128)(2,1)} %wd.7, f32[512,1]{1,0:T(8,128)} %reshape.230.scale), custom_call_target="tpu_custom_call" | custom-call | flops 7516192768 | bytes 22020096 | tf_op jit(solution)/shard_map/pallas_call | solution.py:166
  260.4 6.1 %collective-permute-done.14 = bf16[4,2,32,1792]{3,2,0,1:T(8,128)(2,1)} collective-permute-done((bf16[4,2,32,1792]{3,2,0,1:T(8,128)(2,1)}, bf16[4,2,32,1792]{3,2,0,1:T(8,128)(2,1)}, u32[]{:S(2)}, u32[]{:S(2)}) %collective-permute-start.14) | collective-permute-done | bytes 917536 | tf_op jit(solution)/shard_map/ppermute | solution.py:32
  268.5 13.6 %collective-permute-done.16 = bf16[2,4,32,1792]{3,2,1,0:T(8,128)(2,1)S(1)} collective-permute-done((bf16[2,4,32,1792]{3,2,1,0:T(8,128)(2,1)S(1)}, bf16[2,4,32,1792]{3,2,1,0:T(8,128)(2,1)S(1)}, u32[]{:S(2)}, u32[]{:S(2)}) %collective-permute-start.16) | collective-permute-done | bytes 917536 | tf_op jit(solution)/shard_map/ppermute | solution.py:32
  282.4 9.5 %collective-permute-done.15 = bf16[4,32,1792]{2,1,0:T(8,128)(2,1)S(1)} collective-permute-done((bf16[4,32,1792]{2,1,0:T(8,128)(2,1)S(1)}, bf16[4,32,1792]{2,1,0:T(8,128)(2,1)S(1)}, u32[]{:S(2)}, u32[]{:S(2)}) %collective-permute-start.15) | collective-permute-done | bytes 458784 | tf_op jit(solution)/shard_map/ppermute | solution.py:32
  296.6 5.5 %collective-permute-start.19 = (bf16[32,3584]{1,0:T(8,128)(2,1)S(1)}, bf16[32,3584]{1,0:T(8,128)(2,1)S(1)}, u32[]{:S(2)}, u32[]{:S(2)}) collective-permute-start(bf16[32,3584]{1,0:T(8,128)(2,1)S(1)} %get-tuple-element.51), channel_id=1, source_target_pairs={{0,16},{8,24},{16,0},{24,8},{1,17},{9,25},{17,1},{25,9},{2,18},{10... | collective-permute-start | bytes 688136 | tf_op jit(solution)/shard_map/ppermute | solution.py:32
  304.4 11.3 %collective-permute-done.19 = bf16[32,3584]{1,0:T(8,128)(2,1)S(1)} collective-permute-done((bf16[32,3584]{1,0:T(8,128)(2,1)S(1)}, bf16[32,3584]{1,0:T(8,128)(2,1)S(1)}, u32[]{:S(2)}, u32[]{:S(2)}) %collective-permute-start.19) | collective-permute-done | bytes 229408 | tf_op jit(solution)/shard_map/ppermute | solution.py:32
  315.7 5.7 %collective-permute-done.18 = bf16[32,3584]{1,0:T(8,128)(2,1)S(1)} collective-permute-done((bf16[32,3584]{1,0:T(8,128)(2,1)S(1)}, bf16[32,3584]{1,0:T(8,128)(2,1)S(1)}, u32[]{:S(2)}, u32[]{:S(2)}) %collective-permute-start.18) | collective-permute-done | bytes 229408 | tf_op jit(solution)/shard_map/ppermute | solution.py:32
  324.1 23.4 %shard_map.68.hidden = bf16[512,1024]{1,0:T(8,128)(2,1)} custom-call(s32[2]{0:T(128)} %pad_add_fusion.place, bf16[4,2,2,2,64,3584]{5,4,3,2,1,0:T(8,128)(2,1)} %bitcast.234, bf16[4,2,2,2,64,3584]{5,4,3,2,1,0:T(8,128)(2,1)} %bitcast.235, bf16[1,7168,1024]{2,1,0:T(8,128)(2,1)} %refs_2_.7, bf16[1,7168,1024]{2,1,0:T(8,128)(2,1)} %refs_3_.7), custom_call_target="tpu_custom_call" | custom-call | flops 15032385536 | bytes 36700160 | tf_op jit(solution)/shard_map/pallas_call | solution.py:146
  347.5 13.3 %shard_map.69 = (bf16[2,256,3584]{2,1,0:T(8,128)(2,1)}, bf16[2,256,3584]{2,1,0:T(8,128)(2,1)}) custom-call(s32[2]{0:T(128)} %pad_add_fusion.place, bf16[512,1024]{1,0:T(8,128)(2,1)} %shard_map.68.hidden, bf16[1,1024,7168]{2,1,0:T(8,128)(2,1)} %wd.7, f32[512,1]{1,0:T(8,128)} %reshape.231.scale), custom_call_target="tpu_custom_call" | custom-call | flops 7516192768 | bytes 22020096 | tf_op jit(solution)/shard_map/pallas_call | solution.py:166
  367.4 9.7 %collective-permute-done.33 = bf16[4,32,1792]{2,1,0:T(8,128)(2,1)S(1)} collective-permute-done((bf16[4,32,1792]{2,1,0:T(8,128)(2,1)S(1)}, bf16[4,32,1792]{2,1,0:T(8,128)(2,1)S(1)}, u32[]{:S(2)}, u32[]{:S(2)}) %collective-permute-start.33) | collective-permute-done | bytes 458784 | tf_op jit(solution)/shard_map/ppermute | solution.py:32
  382.2 23.6 %shard_map.70.hidden = bf16[512,1024]{1,0:T(8,128)(2,1)} custom-call(s32[2]{0:T(128)} %pad_add_fusion.place, bf16[4,2,2,2,64,3584]{5,4,3,2,1,0:T(8,128)(2,1)} %bitcast.236, bf16[4,2,2,2,64,3584]{5,4,3,2,1,0:T(8,128)(2,1)} %bitcast.237, bf16[1,7168,1024]{2,1,0:T(8,128)(2,1)} %refs_2_.7, bf16[1,7168,1024]{2,1,0:T(8,128)(2,1)} %refs_3_.7), custom_call_target="tpu_custom_call" | custom-call | flops 15032385536 | bytes 36700160 | tf_op jit(solution)/shard_map/pallas_call | solution.py:146
  405.7 4.0 add_convert_fusion.1
  411.2 13.2 %shard_map.71 = (bf16[2,256,3584]{2,1,0:T(8,128)(2,1)}, bf16[2,256,3584]{2,1,0:T(8,128)(2,1)}) custom-call(s32[2]{0:T(128)} %pad_add_fusion.place, bf16[512,1024]{1,0:T(8,128)(2,1)} %shard_map.70.hidden, bf16[1,1024,7168]{2,1,0:T(8,128)(2,1)} %wd.7, f32[512,1]{1,0:T(8,128)} %reshape.232.scale), custom_call_target="tpu_custom_call" | custom-call | flops 7516192768 | bytes 22020096 | tf_op jit(solution)/shard_map/pallas_call | solution.py:166
  431.3 17.8 %collective-permute-done.40 = bf16[2,4,32,1792]{3,2,1,0:T(8,128)(2,1)S(1)} collective-permute-done((bf16[2,4,32,1792]{3,2,1,0:T(8,128)(2,1)S(1)}, bf16[2,4,32,1792]{3,2,1,0:T(8,128)(2,1)S(1)}, u32[]{:S(2)}, u32[]{:S(2)}) %collective-permute-start.40) | collective-permute-done | bytes 917536 | tf_op jit(solution)/shard_map/ppermute | solution.py:32
  452.4 9.0 %collective-permute-done.41 = bf16[4,32,1792]{2,1,0:T(8,128)(2,1)S(1)} collective-permute-done((bf16[4,32,1792]{2,1,0:T(8,128)(2,1)S(1)}, bf16[4,32,1792]{2,1,0:T(8,128)(2,1)S(1)}, u32[]{:S(2)}, u32[]{:S(2)}) %collective-permute-start.41) | collective-permute-done | bytes 458784 | tf_op jit(solution)/shard_map/ppermute | solution.py:32
  469.1 14.2 %collective-permute-done.46 = bf16[4,2,32,1792]{3,2,0,1:T(8,128)(2,1)S(1)} collective-permute-done((bf16[4,2,32,1792]{3,2,0,1:T(8,128)(2,1)S(1)}, bf16[4,2,32,1792]{3,2,0,1:T(8,128)(2,1)S(1)}, u32[]{:S(2)}, u32[]{:S(2)}) %collective-permute-start.46) | collective-permute-done | bytes 917536 | tf_op jit(solution)/shard_map/ppermute | solution.py:32
  485.4 8.5 %collective-permute-done.47 = bf16[4,32,1792]{2,1,0:T(8,128)(2,1)S(1)} collective-permute-done((bf16[4,32,1792]{2,1,0:T(8,128)(2,1)S(1)}, bf16[4,32,1792]{2,1,0:T(8,128)(2,1)S(1)}, u32[]{:S(2)}, u32[]{:S(2)}) %collective-permute-start.47) | collective-permute-done | bytes 458784 | tf_op jit(solution)/shard_map/ppermute | solution.py:32
  499.7 13.9 %collective-permute-done.51 = bf16[32,3584]{1,0:T(8,128)(2,1)S(1)} collective-permute-done((bf16[32,3584]{1,0:T(8,128)(2,1)S(1)}, bf16[32,3584]{1,0:T(8,128)(2,1)S(1)}, u32[]{:S(2)}, u32[]{:S(2)}) %collective-permute-start.51) | collective-permute-done | bytes 229408 | tf_op jit(solution)/shard_map/ppermute | solution.py:32
  513.6 4.0 collective-permute-done.50
  (192 shorter events, 105.2 us)
Async XLA Ops:
  6.5 317.5 %all-gather.3.cloned.1.call-start = ((), (), s32[]{:S(2)}) async-start(), calls=%async_computation | async-start | bytes 15138816 | tf_op jit(solution)/shard_map/all_gather | solution.py:222
  9.7 21.7 %collective-permute-start.1 = (bf16[32,3584]{1,0:T(8,128)(2,1)S(1)}, bf16[32,3584]{1,0:T(8,128)(2,1)S(1)}, u32[]{:S(2)}, u32[]{:S(2)}) collective-permute-start(bf16[32,3584]{1,0:T(8,128)(2,1)S(1)} %get-tuple-element.63), channel_id=1, source_target_pairs={{0,16},{8,24},{16,0},{24,8},{1,17},{9,25},{17,1},{25,9},{2,18},{10... | collective-permute-start | bytes 688136 | tf_op jit(solution)/shard_map/ppermute | solution.py:32
  12.0 29.1 %collective-permute-start = (bf16[32,3584]{1,0:T(8,128)(2,1)S(1)}, bf16[32,3584]{1,0:T(8,128)(2,1)S(1)}, u32[]{:S(2)}, u32[]{:S(2)}) collective-permute-start(bf16[32,3584]{1,0:T(8,128)(2,1)S(1)} %get-tuple-element.63), channel_id=1, source_target_pairs={{0,8},{8,16},{16,24},{24,0},{1,9},{9,17},{17,25},{25,1},{2,10},{10... | collective-permute-start | bytes 688136 | tf_op jit(solution)/shard_map/ppermute | solution.py:32
  53.9 32.0 %collective-permute-start.6 = (bf16[2,4,32,1792]{3,2,1,0:T(8,128)(2,1)S(1)}, bf16[2,4,32,1792]{3,2,1,0:T(8,128)(2,1)S(1)}, u32[]{:S(2)}, u32[]{:S(2)}) collective-permute-start(bf16[2,4,32,1792]{3,2,1,0:T(8,128)(2,1)S(1)} %get-tuple-element.60), channel_id=1, source_target_pairs={{0,2},{1,3},{2,0},{3,1},{4,6},{5,7},{6,4},{7,5},{8,10},{9,11},{10,... | collective-permute-start | bytes 2752520 | tf_op jit(solution)/shard_map/ppermute | solution.py:32
  56.7 29.2 %collective-permute-start.4 = (bf16[4,2,32,1792]{3,2,0,1:T(8,128)(2,1)S(1)}, bf16[4,2,32,1792]{3,2,0,1:T(8,128)(2,1)S(1)}, u32[]{:S(2)}, u32[]{:S(2)}) collective-permute-start(bf16[4,2,32,1792]{3,2,0,1:T(8,128)(2,1)S(1)} %get-tuple-element.54), channel_id=1, source_target_pairs={{0,4},{4,0},{1,5},{5,1},{2,6},{6,2},{3,7},{7,3},{8,12},{12,8},{9,1... | collective-permute-start | bytes 2752520 | tf_op jit(solution)/shard_map/ppermute | solution.py:32
  87.9 86.0 %collective-permute-start.7 = (bf16[2,4,2,32,3584]{4,3,2,1,0:T(8,128)(2,1)}, bf16[2,4,2,32,3584]{4,3,2,1,0:T(8,128)(2,1)}, u32[]{:S(2)}, u32[]{:S(2)}) collective-permute-start(bf16[2,4,2,32,3584]{4,3,2,1,0:T(8,128)(2,1)} %maximum_maximum_fusion.refs_0_), channel_id=1, source_target_pairs={{0,1},{1,0},{2,3},{3,2},{4,5},{5,4},{6,7},{7,6},{8,9},{9,8},{10,11... | collective-permute-start | bytes 11010056 | tf_op jit(solution)/shard_map/ppermute | solution.py:32
  90.3 21.9 %collective-permute-start.23 = (bf16[32,3584]{1,0:T(8,128)(2,1)S(1)}, bf16[32,3584]{1,0:T(8,128)(2,1)S(1)}, u32[]{:S(2)}, u32[]{:S(2)}) collective-permute-start(bf16[32,3584]{1,0:T(8,128)(2,1)S(1)} %get-tuple-element.64), channel_id=1, source_target_pairs={{0,24},{8,0},{16,8},{24,16},{1,25},{9,1},{17,9},{25,17},{2,26},{10... | collective-permute-start | bytes 688136 | tf_op jit(solution)/shard_map/ppermute | solution.py:32
  90.3 24.3 %collective-permute-start.22 = (bf16[32,3584]{1,0:T(8,128)(2,1)S(1)}, bf16[32,3584]{1,0:T(8,128)(2,1)S(1)}, u32[]{:S(2)}, u32[]{:S(2)}) collective-permute-start(bf16[32,3584]{1,0:T(8,128)(2,1)S(1)} %get-tuple-element.64), channel_id=1, source_target_pairs={{0,16},{8,24},{16,0},{24,8},{1,17},{9,25},{17,1},{25,9},{2,18},{10... | collective-permute-start | bytes 688136 | tf_op jit(solution)/shard_map/ppermute | solution.py:32
  93.8 38.8 %collective-permute-start.21 = (bf16[32,3584]{1,0:T(8,128)(2,1)S(1)}, bf16[32,3584]{1,0:T(8,128)(2,1)S(1)}, u32[]{:S(2)}, u32[]{:S(2)}) collective-permute-start(bf16[32,3584]{1,0:T(8,128)(2,1)S(1)} %get-tuple-element.64), channel_id=1, source_target_pairs={{0,8},{8,16},{16,24},{24,0},{1,9},{9,17},{17,25},{25,1},{2,10},{10... | collective-permute-start | bytes 688136 | tf_op jit(solution)/shard_map/ppermute | solution.py:32
  144.6 25.8 %collective-permute-start.27 = (bf16[2,4,32,1792]{3,2,1,0:T(8,128)(2,1)}, bf16[2,4,32,1792]{3,2,1,0:T(8,128)(2,1)S(1)}, u32[]{:S(2)}, u32[]{:S(2)}) collective-permute-start(bf16[2,4,32,1792]{3,2,1,0:T(8,128)(2,1)} %get-tuple-element.72), channel_id=1, source_target_pairs={{0,2},{1,3},{2,0},{3,1},{4,6},{5,7},{6,4},{7,5},{8,10},{9,11},{10,... | collective-permute-start | bytes 2752520 | tf_op jit(solution)/shard_map/ppermute | solution.py:32
  146.1 24.3 %collective-permute-start.25 = (bf16[4,2,32,1792]{3,2,0,1:T(8,128)(2,1)}, bf16[4,2,32,1792]{3,2,0,1:T(8,128)(2,1)}, u32[]{:S(2)}, u32[]{:S(2)}) collective-permute-start(bf16[4,2,32,1792]{3,2,0,1:T(8,128)(2,1)} %get-tuple-element.66), channel_id=1, source_target_pairs={{0,4},{4,0},{1,5},{5,1},{2,6},{6,2},{3,7},{7,3},{8,12},{12,8},{9,1... | collective-permute-start | bytes 2752520 | tf_op jit(solution)/shard_map/ppermute | solution.py:32
  173.5 41.5 %collective-permute-start.28 = (bf16[2,4,2,32,3584]{4,3,2,1,0:T(8,128)(2,1)}, bf16[2,4,2,32,3584]{4,3,2,1,0:T(8,128)(2,1)}, u32[]{:S(2)}, u32[]{:S(2)}) collective-permute-start(bf16[2,4,2,32,3584]{4,3,2,1,0:T(8,128)(2,1)} %maximum_maximum_fusion.1.refs_0_), channel_id=1, source_target_pairs={{0,1},{1,0},{2,3},{3,2},{4,5},{5,4},{6,7},{7,6},{8,9},{9,8},{10,11... | collective-permute-start | bytes 11010056 | tf_op jit(solution)/shard_map/ppermute | solution.py:32
  210.4 27.8 %collective-permute-start.13 = (bf16[2,256,3584]{2,1,0:T(8,128)(2,1)}, bf16[2,256,3584]{2,1,0:T(8,128)(2,1)}, u32[]{:S(2)}, u32[]{:S(2)}) collective-permute-start(bf16[2,256,3584]{2,1,0:T(8,128)(2,1)} %get-tuple-element.20), channel_id=1, source_target_pairs={{0,1},{1,0},{2,3},{3,2},{4,5},{5,4},{6,7},{7,6},{8,9},{9,8},{10,11... | collective-permute-start | bytes 11010056 | tf_op jit(solution)/shard_map/ppermute | solution.py:32
  244.3 22.2 %collective-permute-start.14 = (bf16[4,2,32,1792]{3,2,0,1:T(8,128)(2,1)}, bf16[4,2,32,1792]{3,2,0,1:T(8,128)(2,1)}, u32[]{:S(2)}, u32[]{:S(2)}) collective-permute-start(bf16[4,2,32,1792]{3,2,0,1:T(8,128)(2,1)} %bitcast.232), channel_id=1, source_target_pairs={{0,4},{4,0},{1,5},{5,1},{2,6},{6,2},{3,7},{7,3},{8,12},{12,8},{9,1... | collective-permute-start | bytes 2752520 | tf_op jit(solution)/shard_map/ppermute | solution.py:32
  259.4 42.7 %collective-permute-start.29 = (bf16[2,256,3584]{2,1,0:T(8,128)(2,1)}, bf16[2,256,3584]{2,1,0:T(8,128)(2,1)S(1)}, u32[]{:S(2)}, u32[]{:S(2)}) collective-permute-start(bf16[2,256,3584]{2,1,0:T(8,128)(2,1)} %get-tuple-element.24), channel_id=1, source_target_pairs={{0,1},{1,0},{2,3},{3,2},{4,5},{5,4},{6,7},{7,6},{8,9},{9,8},{10,11... | collective-permute-start | bytes 11010056 | tf_op jit(solution)/shard_map/ppermute | solution.py:32
  260.1 22.0 %collective-permute-start.16 = (bf16[2,4,32,1792]{3,2,1,0:T(8,128)(2,1)S(1)}, bf16[2,4,32,1792]{3,2,1,0:T(8,128)(2,1)S(1)}, u32[]{:S(2)}, u32[]{:S(2)}) collective-permute-start(bf16[2,4,32,1792]{3,2,1,0:T(8,128)(2,1)S(1)} %slice_bitcast_fusion.2), channel_id=1, source_target_pairs={{0,2},{1,3},{2,0},{3,1},{4,6},{5,7},{6,4},{7,5},{8,10},{9,11},{10,... | collective-permute-start | bytes 2752520 | tf_op jit(solution)/shard_map/ppermute | solution.py:32
  268.2 23.7 %collective-permute-start.15 = (bf16[4,32,1792]{2,1,0:T(8,128)(2,1)S(1)}, bf16[4,32,1792]{2,1,0:T(8,128)(2,1)S(1)}, u32[]{:S(2)}, u32[]{:S(2)}) collective-permute-start(bf16[4,32,1792]{2,1,0:T(8,128)(2,1)S(1)} %slice_bitcast_fusion.14), channel_id=1, source_target_pairs={{0,2},{1,3},{2,0},{3,1},{4,6},{5,7},{6,4},{7,5},{8,10},{9,11},{10,... | collective-permute-start | bytes 1376264 | tf_op jit(solution)/shard_map/ppermute | solution.py:32
  322.2 41.3 %collective-permute-start.32 = (bf16[2,4,32,1792]{3,2,1,0:T(8,128)(2,1)S(1)}, bf16[2,4,32,1792]{3,2,1,0:T(8,128)(2,1)S(1)}, u32[]{:S(2)}, u32[]{:S(2)}) collective-permute-start(bf16[2,4,32,1792]{3,2,1,0:T(8,128)(2,1)S(1)} %slice_bitcast_fusion), channel_id=1, source_target_pairs={{0,2},{1,3},{2,0},{3,1},{4,6},{5,7},{6,4},{7,5},{8,10},{9,11},{10,... | collective-permute-start | bytes 2752520 | tf_op jit(solution)/shard_map/ppermute | solution.py:32
  322.8 43.5 %collective-permute-start.31 = (bf16[4,32,1792]{2,1,0:T(8,128)(2,1)S(1)}, bf16[4,32,1792]{2,1,0:T(8,128)(2,1)}, u32[]{:S(2)}, u32[]{:S(2)}) collective-permute-start(bf16[4,32,1792]{2,1,0:T(8,128)(2,1)S(1)} %slice_bitcast_fusion.10), channel_id=1, source_target_pairs={{0,2},{1,3},{2,0},{3,1},{4,6},{5,7},{6,4},{7,5},{8,10},{9,11},{10,... | collective-permute-start | bytes 1376264 | tf_op jit(solution)/shard_map/ppermute | solution.py:32
  360.8 44.9 %collective-permute-start.37 = (bf16[2,256,3584]{2,1,0:T(8,128)(2,1)}, bf16[2,256,3584]{2,1,0:T(8,128)(2,1)}, u32[]{:S(2)}, u32[]{:S(2)}) collective-permute-start(bf16[2,256,3584]{2,1,0:T(8,128)(2,1)} %get-tuple-element.28), channel_id=1, source_target_pairs={{0,1},{1,0},{2,3},{3,2},{4,5},{5,4},{6,7},{7,6},{8,9},{9,8},{10,11... | collective-permute-start | bytes 11010056 | tf_op jit(solution)/shard_map/ppermute | solution.py:32
  378.9 49.7 %collective-permute-start.36 = (bf16[32,3584]{1,0:T(8,128)(2,1)}, bf16[32,3584]{1,0:T(8,128)(2,1)}, u32[]{:S(2)}, u32[]{:S(2)}) collective-permute-start(bf16[32,3584]{1,0:T(8,128)(2,1)} %get-tuple-element.42), channel_id=1, source_target_pairs={{0,8},{8,16},{16,24},{24,0},{1,9},{9,17},{17,25},{25,1},{2,10},{10... | collective-permute-start | bytes 688136 | tf_op jit(solution)/shard_map/ppermute | solution.py:32
  380.4 48.2 %collective-permute-start.35 = (bf16[32,3584]{1,0:T(8,128)(2,1)}, bf16[32,3584]{1,0:T(8,128)(2,1)}, u32[]{:S(2)}, u32[]{:S(2)}) collective-permute-start(bf16[32,3584]{1,0:T(8,128)(2,1)} %get-tuple-element.43), channel_id=1, source_target_pairs={{0,16},{8,24},{16,0},{24,8},{1,17},{9,25},{17,1},{25,9},{2,18},{10... | collective-permute-start | bytes 688136 | tf_op jit(solution)/shard_map/ppermute | solution.py:32
  382.2 46.4 %collective-permute-start.34 = (bf16[32,3584]{1,0:T(8,128)(2,1)}, bf16[32,3584]{1,0:T(8,128)(2,1)}, u32[]{:S(2)}, u32[]{:S(2)}) collective-permute-start(bf16[32,3584]{1,0:T(8,128)(2,1)} %get-tuple-element.41), channel_id=1, source_target_pairs={{0,24},{8,0},{16,8},{24,16},{1,25},{9,1},{17,9},{25,17},{2,26},{10... | collective-permute-start | bytes 688136 | tf_op jit(solution)/shard_map/ppermute | solution.py:32
  424.5 37.1 %collective-permute-start.45 = (bf16[2,256,3584]{2,1,0:T(8,128)(2,1)}, bf16[2,256,3584]{2,1,0:T(8,128)(2,1)S(1)}, u32[]{:S(2)}, u32[]{:S(2)}) collective-permute-start(bf16[2,256,3584]{2,1,0:T(8,128)(2,1)} %get-tuple-element.32), channel_id=1, source_target_pairs={{0,1},{1,0},{2,3},{3,2},{4,5},{5,4},{6,7},{7,6},{8,9},{9,8},{10,11... | collective-permute-start | bytes 11010056 | tf_op jit(solution)/shard_map/ppermute | solution.py:32
  427.2 22.0 %collective-permute-start.40 = (bf16[2,4,32,1792]{3,2,1,0:T(8,128)(2,1)S(1)}, bf16[2,4,32,1792]{3,2,1,0:T(8,128)(2,1)S(1)}, u32[]{:S(2)}, u32[]{:S(2)}) collective-permute-start(bf16[2,4,32,1792]{3,2,1,0:T(8,128)(2,1)S(1)} %dynamic-slice_bitcast_fusion.1), channel_id=1, source_target_pairs={{0,2},{1,3},{2,0},{3,1},{4,6},{5,7},{6,4},{7,5},{8,10},{9,11},{10,... | collective-permute-start | bytes 2752520 | tf_op jit(solution)/shard_map/ppermute | solution.py:32
  430.1 21.7 %collective-permute-start.38 = (bf16[4,2,32,1792]{3,2,0,1:T(8,128)(2,1)S(1)}, bf16[4,2,32,1792]{3,2,0,1:T(8,128)(2,1)S(1)}, u32[]{:S(2)}, u32[]{:S(2)}) collective-permute-start(bf16[4,2,32,1792]{3,2,0,1:T(8,128)(2,1)S(1)} %bitcast.253), channel_id=1, source_target_pairs={{0,4},{4,0},{1,5},{5,1},{2,6},{6,2},{3,7},{7,3},{8,12},{12,8},{9,1... | collective-permute-start | bytes 2752520 | tf_op jit(solution)/shard_map/ppermute | solution.py:32
  462.7 20.6 %collective-permute-start.46 = (bf16[4,2,32,1792]{3,2,0,1:T(8,128)(2,1)S(1)}, bf16[4,2,32,1792]{3,2,0,1:T(8,128)(2,1)S(1)}, u32[]{:S(2)}, u32[]{:S(2)}) collective-permute-start(bf16[4,2,32,1792]{3,2,0,1:T(8,128)(2,1)S(1)} %bitcast.251), channel_id=1, source_target_pairs={{0,4},{4,0},{1,5},{5,1},{2,6},{6,2},{3,7},{7,3},{8,12},{12,8},{9,1... | collective-permute-start | bytes 2752520 | tf_op jit(solution)/shard_map/ppermute | solution.py:32
  464.1 20.2 %collective-permute-start.48 = (bf16[2,4,32,1792]{3,2,1,0:T(8,128)(2,1)S(1)}, bf16[2,4,32,1792]{3,2,1,0:T(8,128)(2,1)S(1)}, u32[]{:S(2)}, u32[]{:S(2)}) collective-permute-start(bf16[2,4,32,1792]{3,2,1,0:T(8,128)(2,1)S(1)} %dynamic-slice_bitcast_fusion), channel_id=1, source_target_pairs={{0,2},{1,3},{2,0},{3,1},{4,6},{5,7},{6,4},{7,5},{8,10},{9,11},{10,... | collective-permute-start | bytes 2752520 | tf_op jit(solution)/shard_map/ppermute | solution.py:32
  465.0 33.4 %collective-permute-start.44 = (bf16[32,3584]{1,0:T(8,128)(2,1)S(1)}, bf16[32,3584]{1,0:T(8,128)(2,1)S(1)}, u32[]{:S(2)}, u32[]{:S(2)}) collective-permute-start(bf16[32,3584]{1,0:T(8,128)(2,1)S(1)} %get-tuple-element.46), channel_id=1, source_target_pairs={{0,8},{8,16},{16,24},{24,0},{1,9},{9,17},{17,25},{25,1},{2,10},{10... | collective-permute-start | bytes 688136 | tf_op jit(solution)/shard_map/ppermute | solution.py:32
  466.8 31.6 %collective-permute-start.43 = (bf16[32,3584]{1,0:T(8,128)(2,1)S(1)}, bf16[32,3584]{1,0:T(8,128)(2,1)S(1)}, u32[]{:S(2)}, u32[]{:S(2)}) collective-permute-start(bf16[32,3584]{1,0:T(8,128)(2,1)S(1)} %get-tuple-element.45), channel_id=1, source_target_pairs={{0,16},{8,24},{16,0},{24,8},{1,17},{9,25},{17,1},{25,9},{2,18},{10... | collective-permute-start | bytes 688136 | tf_op jit(solution)/shard_map/ppermute | solution.py:32
  469.1 29.3 %collective-permute-start.42 = (bf16[32,3584]{1,0:T(8,128)(2,1)S(1)}, bf16[32,3584]{1,0:T(8,128)(2,1)S(1)}, u32[]{:S(2)}, u32[]{:S(2)}) collective-permute-start(bf16[32,3584]{1,0:T(8,128)(2,1)S(1)} %get-tuple-element.44), channel_id=1, source_target_pairs={{0,24},{8,0},{16,8},{24,16},{1,25},{9,1},{17,9},{25,17},{2,26},{10... | collective-permute-start | bytes 688136 | tf_op jit(solution)/shard_map/ppermute | solution.py:32
  498.4 19.2 %collective-permute-start.50 = (bf16[32,3584]{1,0:T(8,128)(2,1)S(1)}, bf16[32,3584]{1,0:T(8,128)(2,1)S(1)}, u32[]{:S(2)}, u32[]{:S(2)}) collective-permute-start(bf16[32,3584]{1,0:T(8,128)(2,1)S(1)} %get-tuple-element.47), channel_id=1, source_target_pairs={{0,24},{8,0},{16,8},{24,16},{1,25},{9,1},{17,9},{25,17},{2,26},{10... | collective-permute-start | bytes 688136 | tf_op jit(solution)/shard_map/ppermute | solution.py:32
  (30 other events, 410.1 us)
Sparse Core Ops, SparseCore 0:
  10.2 140.7 all-gather.2

commit v3 on v2

--- a/solution.py
+++ b/solution.py
@@ -115,7 +115,8 @@
     weight = route_scale * codes / jnp.sum(codes, axis=1, keepdims=True)
     named = routing[None, :, :] == jnp.arange(experts, dtype=jnp.int32)[:, None, None]
     scores = jnp.sum(jnp.where(named, weight[None, :, :], 0.0), axis=2)
-    scores = wide.gather(zed.gather(scores))
+    scores = zed.gather(scores)
+    scores = wide.gather(scores)
     scores = pair.gather(scores)
     own = jnp.arange(experts, dtype=jnp.int32)[:, None] == mine
     scores = jnp.sum(jnp.where(own, scores, 0.0), axis=3)
@@ -184,7 +185,7 @@
             compiler_params=pltpu.CompilerParams(vmem_limit_bytes=60 * 1024 * 1024),
         )(place, hidden, w_down, scale)
 
-    def give_back(outs, moving):
+    def give_back(outs, moving, wait, hold):
         arrived = pair.send(outs)
         yield []
         value = total_of(outs[0], arrived).reshape(n_ba, n_aa, n_high, rows, width)
@@ -194,6 +195,9 @@
         walls = wide.blocks(second, 2, moving)
         got_a, got_b = feat.send(sides), wide.send(walls)
         yield [value]
+        if wait:
+            held = lax.optimization_barrier((*got_a, *got_b, *wait))
+            got_a, got_b = held[: len(got_a)], held[len(got_a) : len(got_a) + len(got_b)]
         first = total_of(sides[0], got_a)
         second = total_of(walls[0], got_b)
         walls = wide.blocks(first, 1, moving)
@@ -204,6 +208,8 @@
         floors = zed.blocks(value, 0, moving)
         arrived = zed.send(floors)
         yield [value]
+        if hold:
+            arrived = lax.optimization_barrier((*arrived, *hold))[: len(arrived)]
         yield [total_of(floors[0], arrived)]
 
     def walk(piece):
@@ -228,7 +234,7 @@
     def tie(value, others):
         return lax.optimization_barrier((value, *others))[0] if others else value
 
-    sums, last = [], {}
+    sums, last, hold, waits = [], {}, [], [[] for _ in range(n_calls)]
 
     def step(number):
         last[number] = next(sums[number])
@@ -242,12 +248,16 @@
         hidden = hidden_of([first] + others, max(number - n_walked, 0))
         between = [v for back in (3, 2, 1) if number >= back for v in step(number - back)]
         outs = list(out_of(tie(hidden, between), number))
-        sums.append(give_back(outs, number >= n_walked))
+        sums.append(give_back(outs, number >= n_walked, waits[number], hold))
         step(number)
-    for _ in range(5):
-        for number in range(n_calls):
-            for last[number] in sums[number]:
-                break
+    end = n_calls - 1
+    waits[end - 1].extend(step(end))
+    for number in (end - 2, end - 1, end, end - 1):
+        step(number)
+    hold.extend(step(end))
+    for number in range(n_calls):
+        for last[number] in sums[number]:
+            pass
     return jnp.concatenate([last[c][0] for c in range(n_calls)], axis=0)
 
 

time: 531 us -> 589 us (1.11)
  the two profiles are of different devices: /device:TPU:11 before, /device:TPU:0 now
where the time goes in v3:
time: 589 us; the launch traced here: 585 us
  waiting for transfers between devices  303 us (51%)
  Pallas kernels  157 us (27%)
  starting transfers between devices  62.2 us (11%)
  other arithmetic  32.2 us (5%)
  local copies, waits for them, and re-layouts  16.5 us (3%)
  between operations  14.2 us (2%)
    ppermute x53, waiting for transfers between devices, shift(): return lax.ppermute(value, self.axis, pairs)  303 us
    pallas_call x4, Pallas kernels, hidden_of(): pl.pallas_call(functools.partial(hidden_body, steps), grid_spec=pltpu.Pre...  93.2 us
    pallas_call x4, Pallas kernels, out_of(): pl.pallas_call(down_body, grid_spec=pltpu.PrefetchScalarGridSpec(num_scal...  63.6 us
    ppermute x53, starting transfers between devices, shift(): return lax.ppermute(value, self.axis, pairs)  62.2 us
    convert_element_type x24, other arithmetic, total_of(): return total.astype(jnp.bfloat16)  21.1 us
  transfers between devices with their start and end apart: 54, of which 28 were waited for; matrix products, arithmetic and copies ran while one was open for 6% of the time, Pallas kernels for 25%

profile of v3, /device:TPU:0, one launch (start us, length us, event | category | flops | bytes accessed | tf_op | source)
XLA Modules:
  0.0 584.9 jit_solution(3091497934074279203)
XLA Ops:
  9.5 5.1 collective-permute-start.2
  15.6 5.0 collective-permute-done.2
  20.6 23.3 %collective-permute-done.1 = bf16[32,3584]{1,0:T(8,128)(2,1)S(1)} collective-permute-done((bf16[32,3584]{1,0:T(8,128)(2,1)S(1)}, bf16[32,3584]{1,0:T(8,128)(2,1)S(1)}, u32[]{:S(2)}, u32[]{:S(2)}) %collective-permute-start.1) | collective-permute-done | bytes 229408 | tf_op jit(solution)/shard_map/ppermute | solution.py:32
  47.3 10.5 %collective-permute-done.5 = bf16[4,32,1792]{2,1,0:T(8,128)(2,1)S(1)} collective-permute-done((bf16[4,32,1792]{2,1,0:T(8,128)(2,1)S(1)}, bf16[4,32,1792]{2,1,0:T(8,128)(2,1)S(1)}, u32[]{:S(2)}, u32[]{:S(2)}) %collective-permute-start.5) | collective-permute-done | bytes 458784 | tf_op jit(solution)/shard_map/ppermute | solution.py:32
  59.3 5.6 collective-permute-done.3
  65.1 21.9 %collective-permute-done.6 = bf16[2,4,32,1792]{3,2,1,0:T(8,128)(2,1)S(1)} collective-permute-done((bf16[2,4,32,1792]{3,2,1,0:T(8,128)(2,1)S(1)}, bf16[2,4,32,1792]{3,2,1,0:T(8,128)(2,1)S(1)}, u32[]{:S(2)}, u32[]{:S(2)}) %collective-permute-start.6) | collective-permute-done | bytes 917536 | tf_op jit(solution)/shard_map/ppermute | solution.py:32
  89.0 5.8 collective-permute-start.22
  96.8 12.0 %collective-permute-done.23 = bf16[32,3584]{1,0:T(8,128)(2,1)S(1)} collective-permute-done((bf16[32,3584]{1,0:T(8,128)(2,1)S(1)}, bf16[32,3584]{1,0:T(8,128)(2,1)S(1)}, u32[]{:S(2)}, u32[]{:S(2)}) %collective-permute-start.23) | collective-permute-done | bytes 229408 | tf_op jit(solution)/shard_map/ppermute | solution.py:32
  108.8 31.7 %collective-permute-done.22 = bf16[32,3584]{1,0:T(8,128)(2,1)S(1)} collective-permute-done((bf16[32,3584]{1,0:T(8,128)(2,1)S(1)}, bf16[32,3584]{1,0:T(8,128)(2,1)S(1)}, u32[]{:S(2)}, u32[]{:S(2)}) %collective-permute-start.22) | collective-permute-done | bytes 229408 | tf_op jit(solution)/shard_map/ppermute | solution.py:32
  143.0 10.4 %collective-permute-done.26 = bf16[4,32,1792]{2,1,0:T(8,128)(2,1)S(1)} collective-permute-done((bf16[4,32,1792]{2,1,0:T(8,128)(2,1)S(1)}, bf16[4,32,1792]{2,1,0:T(8,128)(2,1)S(1)}, u32[]{:S(2)}, u32[]{:S(2)}) %collective-permute-start.26) | collective-permute-done | bytes 458784 | tf_op jit(solution)/shard_map/ppermute | solution.py:32
  167.2 9.6 %collective-permute-done.11 = f32[4,16,128]{2,1,0:T(8,128)S(1)} collective-permute-done((f32[4,16,128]{2,1,0:T(8,128)S(1)}, f32[4,16,128]{2,1,0:T(8,128)S(1)}, u32[]{:S(2)}, u32[]{:S(2)}) %collective-permute-start.11) | collective-permute-done | bytes 32800 | tf_op jit(solution)/shard_map/ppermute | solution.py:32
  182.9 23.2 %shard_map.64.hidden = bf16[512,1024]{1,0:T(8,128)(2,1)} custom-call(s32[2]{0:T(128)} %pad_add_fusion.place, bf16[2,4,2,32,3584]{4,3,2,1,0:T(8,128)(2,1)} %maximum_maximum_fusion.refs_0_, bf16[2,4,2,32,3584]{4,3,2,1,0:T(8,128)(2,1)} %collective-permute-done.7.refs_1_, bf16[1,7168,1024]{2,1,0:T(8,128)(2,1)} %refs_2_.7, bf16[1,7168,1024]{2,1,0:T(8,128)(2,1)} %refs_3_.7), custom_call_target="tpu_custom_call" | custom-call | flops 15032385536 | bytes 36700160 | tf_op jit(solution)/shard_map/pallas_call | solution.py:147
  206.1 13.3 %shard_map.65 = (bf16[2,256,3584]{2,1,0:T(8,128)(2,1)}, bf16[2,256,3584]{2,1,0:T(8,128)(2,1)}) custom-call(s32[2]{0:T(128)} %pad_add_fusion.place, bf16[512,1024]{1,0:T(8,128)(2,1)} %shard_map.64.hidden, bf16[1,1024,7168]{2,1,0:T(8,128)(2,1)} %wd.7, f32[512,1]{1,0:T(8,128)} %reshape.229.scale), custom_call_target="tpu_custom_call" | custom-call | flops 7516192768 | bytes 22020096 | tf_op jit(solution)/shard_map/pallas_call | solution.py:167
  224.2 23.2 %shard_map.66.hidden = bf16[512,1024]{1,0:T(8,128)(2,1)} custom-call(s32[2]{0:T(128)} %pad_add_fusion.place, bf16[2,4,2,32,3584]{4,3,2,1,0:T(8,128)(2,1)} %maximum_maximum_fusion.1.refs_0_, bf16[2,4,2,32,3584]{4,3,2,1,0:T(8,128)(2,1)} %collective-permute-done.28.refs_1_, bf16[1,7168,1024]{2,1,0:T(8,128)(2,1)} %refs_2_.7, bf16[1,7168,1024]{2,1,0:T(8,128)(2,1)} %refs_3_.7), custom_call_target="tpu_custom_call" | custom-call | flops 15032385536 | bytes 36700160 | tf_op jit(solution)/shard_map/pallas_call | solution.py:147
  254.2 23.2 %shard_map.67 = (bf16[2,256,3584]{2,1,0:T(8,128)(2,1)}, bf16[2,256,3584]{2,1,0:T(8,128)(2,1)}) custom-call(s32[2]{0:T(128)} %pad_add_fusion.place, bf16[512,1024]{1,0:T(8,128)(2,1)} %shard_map.66.hidden, bf16[1,1024,7168]{2,1,0:T(8,128)(2,1)} %wd.7, f32[512,1]{1,0:T(8,128)} %reshape.230.scale), custom_call_target="tpu_custom_call" | custom-call | flops 7516192768 | bytes 22020096 | tf_op jit(solution)/shard_map/pallas_call | solution.py:167
  281.5 19.4 %collective-permute-done.16 = bf16[2,4,32,1792]{3,2,1,0:T(8,128)(2,1)S(1)} collective-permute-done((bf16[2,4,32,1792]{3,2,1,0:T(8,128)(2,1)S(1)}, bf16[2,4,32,1792]{3,2,1,0:T(8,128)(2,1)S(1)}, u32[]{:S(2)}, u32[]{:S(2)}) %collective-permute-start.16) | collective-permute-done | bytes 917536 | tf_op jit(solution)/shard_map/ppermute | solution.py:32
  302.6 7.6 %collective-permute-done.15 = bf16[4,32,1792]{2,1,0:T(8,128)(2,1)S(1)} collective-permute-done((bf16[4,32,1792]{2,1,0:T(8,128)(2,1)S(1)}, bf16[4,32,1792]{2,1,0:T(8,128)(2,1)S(1)}, u32[]{:S(2)}, u32[]{:S(2)}) %collective-permute-start.15) | collective-permute-done | bytes 458784 | tf_op jit(solution)/shard_map/ppermute | solution.py:32
  321.9 23.4 %shard_map.68.hidden = bf16[512,1024]{1,0:T(8,128)(2,1)} custom-call(s32[2]{0:T(128)} %pad_add_fusion.place, bf16[4,2,2,2,64,3584]{5,4,3,2,1,0:T(8,128)(2,1)} %bitcast.234, bf16[4,2,2,2,64,3584]{5,4,3,2,1,0:T(8,128)(2,1)} %bitcast.235, bf16[1,7168,1024]{2,1,0:T(8,128)(2,1)} %refs_2_.7, bf16[1,7168,1024]{2,1,0:T(8,128)(2,1)} %refs_3_.7), custom_call_target="tpu_custom_call" | custom-call | flops 15032385536 | bytes 36700160 | tf_op jit(solution)/shard_map/pallas_call | solution.py:147
  345.3 13.7 %shard_map.69 = (bf16[2,256,3584]{2,1,0:T(8,128)(2,1)}, bf16[2,256,3584]{2,1,0:T(8,128)(2,1)}) custom-call(s32[2]{0:T(128)} %pad_add_fusion.place, bf16[512,1024]{1,0:T(8,128)(2,1)} %shard_map.68.hidden, bf16[1,1024,7168]{2,1,0:T(8,128)(2,1)} %wd.7, f32[512,1]{1,0:T(8,128)} %reshape.231.scale), custom_call_target="tpu_custom_call" | custom-call | flops 7516192768 | bytes 22020096 | tf_op jit(solution)/shard_map/pallas_call | solution.py:167
  365.5 18.8 %collective-permute-done.32 = bf16[2,4,32,1792]{3,2,1,0:T(8,128)(2,1)S(1)} collective-permute-done((bf16[2,4,32,1792]{3,2,1,0:T(8,128)(2,1)S(1)}, bf16[2,4,32,1792]{3,2,1,0:T(8,128)(2,1)S(1)}, u32[]{:S(2)}, u32[]{:S(2)}) %collective-permute-start.32) | collective-permute-done | bytes 917536 | tf_op jit(solution)/shard_map/ppermute | solution.py:32
  385.8 23.4 %shard_map.70.hidden = bf16[512,1024]{1,0:T(8,128)(2,1)} custom-call(s32[2]{0:T(128)} %pad_add_fusion.place, bf16[4,2,2,2,64,3584]{5,4,3,2,1,0:T(8,128)(2,1)} %bitcast.236, bf16[4,2,2,2,64,3584]{5,4,3,2,1,0:T(8,128)(2,1)} %bitcast.237, bf16[1,7168,1024]{2,1,0:T(8,128)(2,1)} %refs_2_.7, bf16[1,7168,1024]{2,1,0:T(8,128)(2,1)} %refs_3_.7), custom_call_target="tpu_custom_call" | custom-call | flops 15032385536 | bytes 36700160 | tf_op jit(solution)/shard_map/pallas_call | solution.py:147
  409.2 5.9 %add_convert_fusion.1 = bf16[2,256,3584]{2,1,0:T(8,128)(2,1)} fusion(bf16[2,256,3584]{2,1,0:T(8,128)(2,1)} %collective-permute-done.37, bf16[2,256,3584]{2,1,0:T(8,128)(2,1)} %get-tuple-element.38), kind=kLoop, calls=%fused_computation.3 | loop fusion | flops 7340032 | bytes 11010048 | tf_op jit(solution)/shard_map/convert_element_type | solution.py:56
  415.1 13.4 %shard_map.71 = (bf16[2,256,3584]{2,1,0:T(8,128)(2,1)}, bf16[2,256,3584]{2,1,0:T(8,128)(2,1)}) custom-call(s32[2]{0:T(128)} %pad_add_fusion.place, bf16[512,1024]{1,0:T(8,128)(2,1)} %shard_map.70.hidden, bf16[1,1024,7168]{2,1,0:T(8,128)(2,1)} %wd.7, f32[512,1]{1,0:T(8,128)} %reshape.232.scale), custom_call_target="tpu_custom_call" | custom-call | flops 7516192768 | bytes 22020096 | tf_op jit(solution)/shard_map/pallas_call | solution.py:167
  430.9 10.6 %collective-permute-done.33 = bf16[4,32,1792]{2,1,0:T(8,128)(2,1)S(1)} collective-permute-done((bf16[4,32,1792]{2,1,0:T(8,128)(2,1)S(1)}, bf16[4,32,1792]{2,1,0:T(8,128)(2,1)S(1)}, u32[]{:S(2)}, u32[]{:S(2)}) %collective-permute-start.33) | collective-permute-done | bytes 458784 | tf_op jit(solution)/shard_map/ppermute | solution.py:32
  453.2 14.2 %collective-permute-done.43 = bf16[4,2,32,1792]{3,2,0,1:T(8,128)(2,1)S(1)} collective-permute-done((bf16[4,2,32,1792]{3,2,0,1:T(8,128)(2,1)S(1)}, bf16[4,2,32,1792]{3,2,0,1:T(8,128)(2,1)S(1)}, u32[]{:S(2)}, u32[]{:S(2)}) %collective-permute-start.43) | collective-permute-done | bytes 917536 | tf_op jit(solution)/shard_map/ppermute | solution.py:32
  470.1 27.0 %collective-permute-done.46 = bf16[4,32,1792]{2,1,0:T(8,128)(2,1)S(1)} collective-permute-done((bf16[4,32,1792]{2,1,0:T(8,128)(2,1)S(1)}, bf16[4,32,1792]{2,1,0:T(8,128)(2,1)S(1)}, u32[]{:S(2)}, u32[]{:S(2)}) %collective-permute-start.46) | collective-permute-done | bytes 458784 | tf_op jit(solution)/shard_map/ppermute | solution.py:32
  498.9 8.9 %collective-permute-done.45 = bf16[4,32,1792]{2,1,0:T(8,128)(2,1)S(1)} collective-permute-done((bf16[4,32,1792]{2,1,0:T(8,128)(2,1)S(1)}, bf16[4,32,1792]{2,1,0:T(8,128)(2,1)S(1)}, u32[]{:S(2)}, u32[]{:S(2)}) %collective-permute-start.45) | collective-permute-done | bytes 458784 | tf_op jit(solution)/shard_map/ppermute | solution.py:32
  512.4 15.9 %collective-permute-done.41 = bf16[2,4,32,1792]{3,2,1,0:T(8,128)(2,1)S(1)} collective-permute-done((bf16[2,4,32,1792]{3,2,1,0:T(8,128)(2,1)S(1)}, bf16[2,4,32,1792]{3,2,1,0:T(8,128)(2,1)S(1)}, u32[]{:S(2)}, u32[]{:S(2)}) %collective-permute-start.41) | collective-permute-done | bytes 917536 | tf_op jit(solution)/shard_map/ppermute | solution.py:32
  530.2 6.5 %collective-permute-done.40 = bf16[4,32,1792]{2,1,0:T(8,128)(2,1)S(1)} collective-permute-done((bf16[4,32,1792]{2,1,0:T(8,128)(2,1)S(1)}, bf16[4,32,1792]{2,1,0:T(8,128)(2,1)S(1)}, u32[]{:S(2)}, u32[]{:S(2)}) %collective-permute-start.40) | collective-permute-done | bytes 458784 | tf_op jit(solution)/shard_map/ppermute | solution.py:32
  538.3 6.9 %collective-permute-done.42 = bf16[4,32,1792]{2,1,0:T(8,128)(2,1)S(1)} collective-permute-done((bf16[4,32,1792]{2,1,0:T(8,128)(2,1)S(1)}, bf16[4,32,1792]{2,1,0:T(8,128)(2,1)S(1)}, u32[]{:S(2)}, u32[]{:S(2)}) %collective-permute-start.42) | collective-permute-done | bytes 458784 | tf_op jit(solution)/shard_map/ppermute | solution.py:32
  548.5 16.0 %collective-permute-done.48 = bf16[32,3584]{1,0:T(8,128)(2,1)S(1)} collective-permute-done((bf16[32,3584]{1,0:T(8,128)(2,1)S(1)}, bf16[32,3584]{1,0:T(8,128)(2,1)S(1)}, u32[]{:S(2)}, u32[]{:S(2)}) %collective-permute-start.48) | collective-permute-done | bytes 229408 | tf_op jit(solution)/shard_map/ppermute | solution.py:32
  571.5 5.2 collective-permute-done.51
  (200 shorter events, 110.0 us)
Async XLA Ops:
  6.5 315.4 %all-gather.3.cloned.1.call-start = ((), (), s32[]{:S(2)}) async-start(), calls=%async_computation | async-start | bytes 15138816 | tf_op jit(solution)/shard_map/all_gather | solution.py:228
  14.6 29.3 %collective-permute-start.1 = (bf16[32,3584]{1,0:T(8,128)(2,1)S(1)}, bf16[32,3584]{1,0:T(8,128)(2,1)S(1)}, u32[]{:S(2)}, u32[]{:S(2)}) collective-permute-start(bf16[32,3584]{1,0:T(8,128)(2,1)S(1)} %get-tuple-element.85), channel_id=1, source_target_pairs={{0,16},{8,24},{16,0},{24,8},{1,17},{9,25},{17,1},{25,9},{2,18},{10... | collective-permute-start | bytes 688136 | tf_op jit(solution)/shard_map/ppermute | solution.py:32
  14.6 29.3 %collective-permute-start = (bf16[32,3584]{1,0:T(8,128)(2,1)S(1)}, bf16[32,3584]{1,0:T(8,128)(2,1)S(1)}, u32[]{:S(2)}, u32[]{:S(2)}) collective-permute-start(bf16[32,3584]{1,0:T(8,128)(2,1)S(1)} %get-tuple-element.85), channel_id=1, source_target_pairs={{0,8},{8,16},{16,24},{24,0},{1,9},{9,17},{17,25},{25,1},{2,10},{10... | collective-permute-start | bytes 688136 | tf_op jit(solution)/shard_map/ppermute | solution.py:32
  57.8 29.1 %collective-permute-start.6 = (bf16[2,4,32,1792]{3,2,1,0:T(8,128)(2,1)S(1)}, bf16[2,4,32,1792]{3,2,1,0:T(8,128)(2,1)S(1)}, u32[]{:S(2)}, u32[]{:S(2)}) collective-permute-start(bf16[2,4,32,1792]{3,2,1,0:T(8,128)(2,1)S(1)} %get-tuple-element.82), channel_id=1, source_target_pairs={{0,2},{1,3},{2,0},{3,1},{4,6},{5,7},{6,4},{7,5},{8,10},{9,11},{10,... | collective-permute-start | bytes 2752520 | tf_op jit(solution)/shard_map/ppermute | solution.py:32
  65.0 22.0 %collective-permute-start.4 = (bf16[4,2,32,1792]{3,2,0,1:T(8,128)(2,1)S(1)}, bf16[4,2,32,1792]{3,2,0,1:T(8,128)(2,1)S(1)}, u32[]{:S(2)}, u32[]{:S(2)}) collective-permute-start(bf16[4,2,32,1792]{3,2,0,1:T(8,128)(2,1)S(1)} %get-tuple-element.76), channel_id=1, source_target_pairs={{0,4},{4,0},{1,5},{5,1},{2,6},{6,2},{3,7},{7,3},{8,12},{12,8},{9,1... | collective-permute-start | bytes 2752520 | tf_op jit(solution)/shard_map/ppermute | solution.py:32
  89.0 93.9 %collective-permute-start.7 = (bf16[2,4,2,32,3584]{4,3,2,1,0:T(8,128)(2,1)}, bf16[2,4,2,32,3584]{4,3,2,1,0:T(8,128)(2,1)}, u32[]{:S(2)}, u32[]{:S(2)}) collective-permute-start(bf16[2,4,2,32,3584]{4,3,2,1,0:T(8,128)(2,1)} %maximum_maximum_fusion.refs_0_), channel_id=1, source_target_pairs={{0,1},{1,0},{2,3},{3,2},{4,5},{5,4},{6,7},{7,6},{8,9},{9,8},{10,11... | collective-permute-start | bytes 11010056 | tf_op jit(solution)/shard_map/ppermute | solution.py:32
  89.0 19.8 %collective-permute-start.23 = (bf16[32,3584]{1,0:T(8,128)(2,1)S(1)}, bf16[32,3584]{1,0:T(8,128)(2,1)S(1)}, u32[]{:S(2)}, u32[]{:S(2)}) collective-permute-start(bf16[32,3584]{1,0:T(8,128)(2,1)S(1)} %get-tuple-element.86), channel_id=1, source_target_pairs={{0,24},{8,0},{16,8},{24,16},{1,25},{9,1},{17,9},{25,17},{2,26},{10... | collective-permute-start | bytes 688136 | tf_op jit(solution)/shard_map/ppermute | solution.py:32
  89.0 51.5 %collective-permute-start.22 = (bf16[32,3584]{1,0:T(8,128)(2,1)S(1)}, bf16[32,3584]{1,0:T(8,128)(2,1)S(1)}, u32[]{:S(2)}, u32[]{:S(2)}) collective-permute-start(bf16[32,3584]{1,0:T(8,128)(2,1)S(1)} %get-tuple-element.86), channel_id=1, source_target_pairs={{0,16},{8,24},{16,0},{24,8},{1,17},{9,25},{17,1},{25,9},{2,18},{10... | collective-permute-start | bytes 688136 | tf_op jit(solution)/shard_map/ppermute | solution.py:32
  94.8 45.7 %collective-permute-start.21 = (bf16[32,3584]{1,0:T(8,128)(2,1)S(1)}, bf16[32,3584]{1,0:T(8,128)(2,1)S(1)}, u32[]{:S(2)}, u32[]{:S(2)}) collective-permute-start(bf16[32,3584]{1,0:T(8,128)(2,1)S(1)} %get-tuple-element.86), channel_id=1, source_target_pairs={{0,8},{8,16},{16,24},{24,0},{1,9},{9,17},{17,25},{25,1},{2,10},{10... | collective-permute-start | bytes 688136 | tf_op jit(solution)/shard_map/ppermute | solution.py:32
  154.4 24.9 %collective-permute-start.27 = (bf16[2,4,32,1792]{3,2,1,0:T(8,128)(2,1)}, bf16[2,4,32,1792]{3,2,1,0:T(8,128)(2,1)S(1)}, u32[]{:S(2)}, u32[]{:S(2)}) collective-permute-start(bf16[2,4,32,1792]{3,2,1,0:T(8,128)(2,1)} %get-tuple-element.94), channel_id=1, source_target_pairs={{0,2},{1,3},{2,0},{3,1},{4,6},{5,7},{6,4},{7,5},{8,10},{9,11},{10,... | collective-permute-start | bytes 2752520 | tf_op jit(solution)/shard_map/ppermute | solution.py:32
  157.1 22.3 %collective-permute-start.25 = (bf16[4,2,32,1792]{3,2,0,1:T(8,128)(2,1)}, bf16[4,2,32,1792]{3,2,0,1:T(8,128)(2,1)}, u32[]{:S(2)}, u32[]{:S(2)}) collective-permute-start(bf16[4,2,32,1792]{3,2,0,1:T(8,128)(2,1)} %get-tuple-element.88), channel_id=1, source_target_pairs={{0,4},{4,0},{1,5},{5,1},{2,6},{6,2},{3,7},{7,3},{8,12},{12,8},{9,1... | collective-permute-start | bytes 2752520 | tf_op jit(solution)/shard_map/ppermute | solution.py:32
  182.7 41.5 %collective-permute-start.28 = (bf16[2,4,2,32,3584]{4,3,2,1,0:T(8,128)(2,1)}, bf16[2,4,2,32,3584]{4,3,2,1,0:T(8,128)(2,1)}, u32[]{:S(2)}, u32[]{:S(2)}) collective-permute-start(bf16[2,4,2,32,3584]{4,3,2,1,0:T(8,128)(2,1)} %maximum_maximum_fusion.1.refs_0_), channel_id=1, source_target_pairs={{0,1},{1,0},{2,3},{3,2},{4,5},{5,4},{6,7},{7,6},{8,9},{9,8},{10,11... | collective-permute-start | bytes 11010056 | tf_op jit(solution)/shard_map/ppermute | solution.py:32
  219.4 28.0 %collective-permute-start.13 = (bf16[2,256,3584]{2,1,0:T(8,128)(2,1)}, bf16[2,256,3584]{2,1,0:T(8,128)(2,1)}, u32[]{:S(2)}, u32[]{:S(2)}) collective-permute-start(bf16[2,256,3584]{2,1,0:T(8,128)(2,1)} %get-tuple-element.31), channel_id=1, source_target_pairs={{0,1},{1,0},{2,3},{3,2},{4,5},{5,4},{6,7},{7,6},{8,9},{9,8},{10,11... | collective-permute-start | bytes 11010056 | tf_op jit(solution)/shard_map/ppermute | solution.py:32
  253.5 25.7 %collective-permute-start.14 = (bf16[4,2,32,1792]{3,2,0,1:T(8,128)(2,1)}, bf16[4,2,32,1792]{3,2,0,1:T(8,128)(2,1)}, u32[]{:S(2)}, u32[]{:S(2)}) collective-permute-start(bf16[4,2,32,1792]{3,2,0,1:T(8,128)(2,1)} %bitcast.232), channel_id=1, source_target_pairs={{0,4},{4,0},{1,5},{5,1},{2,6},{6,2},{3,7},{7,3},{8,12},{12,8},{9,1... | collective-permute-start | bytes 2752520 | tf_op jit(solution)/shard_map/ppermute | solution.py:32
  277.4 40.3 %collective-permute-start.29 = (bf16[2,256,3584]{2,1,0:T(8,128)(2,1)}, bf16[2,256,3584]{2,1,0:T(8,128)(2,1)S(1)}, u32[]{:S(2)}, u32[]{:S(2)}) collective-permute-start(bf16[2,256,3584]{2,1,0:T(8,128)(2,1)} %get-tuple-element.35), channel_id=1, source_target_pairs={{0,1},{1,0},{2,3},{3,2},{4,5},{5,4},{6,7},{7,6},{8,9},{9,8},{10,11... | collective-permute-start | bytes 11010056 | tf_op jit(solution)/shard_map/ppermute | solution.py:32
  277.6 23.3 %collective-permute-start.16 = (bf16[2,4,32,1792]{3,2,1,0:T(8,128)(2,1)S(1)}, bf16[2,4,32,1792]{3,2,1,0:T(8,128)(2,1)S(1)}, u32[]{:S(2)}, u32[]{:S(2)}) collective-permute-start(bf16[2,4,32,1792]{3,2,1,0:T(8,128)(2,1)S(1)} %slice_bitcast_fusion.2), channel_id=1, source_target_pairs={{0,2},{1,3},{2,0},{3,1},{4,6},{5,7},{6,4},{7,5},{8,10},{9,11},{10,... | collective-permute-start | bytes 2752520 | tf_op jit(solution)/shard_map/ppermute | solution.py:32
  281.0 29.2 %collective-permute-start.15 = (bf16[4,32,1792]{2,1,0:T(8,128)(2,1)S(1)}, bf16[4,32,1792]{2,1,0:T(8,128)(2,1)S(1)}, u32[]{:S(2)}, u32[]{:S(2)}) collective-permute-start(bf16[4,32,1792]{2,1,0:T(8,128)(2,1)S(1)} %slice_bitcast_fusion.14), channel_id=1, source_target_pairs={{0,2},{1,3},{2,0},{3,1},{4,6},{5,7},{6,4},{7,5},{8,10},{9,11},{10,... | collective-permute-start | bytes 1376264 | tf_op jit(solution)/shard_map/ppermute | solution.py:32
  313.9 48.1 %collective-permute-start.20 = (bf16[32,3584]{1,0:T(8,128)(2,1)}, bf16[32,3584]{1,0:T(8,128)(2,1)}, u32[]{:S(2)}, u32[]{:S(2)}) collective-permute-start(bf16[32,3584]{1,0:T(8,128)(2,1)} %get-tuple-element.74), channel_id=1, source_target_pairs={{0,8},{8,16},{16,24},{24,0},{1,9},{9,17},{17,25},{25,1},{2,10},{10... | collective-permute-start | bytes 688136 | tf_op jit(solution)/shard_map/ppermute | solution.py:32
  313.9 49.7 %collective-permute-start.19 = (bf16[32,3584]{1,0:T(8,128)(2,1)}, bf16[32,3584]{1,0:T(8,128)(2,1)}, u32[]{:S(2)}, u32[]{:S(2)}) collective-permute-start(bf16[32,3584]{1,0:T(8,128)(2,1)} %get-tuple-element.73), channel_id=1, source_target_pairs={{0,16},{8,24},{16,0},{24,8},{1,17},{9,25},{17,1},{25,9},{2,18},{10... | collective-permute-start | bytes 688136 | tf_op jit(solution)/shard_map/ppermute | solution.py:32
  313.9 49.7 %collective-permute-start.18 = (bf16[32,3584]{1,0:T(8,128)(2,1)}, bf16[32,3584]{1,0:T(8,128)(2,1)}, u32[]{:S(2)}, u32[]{:S(2)}) collective-permute-start(bf16[32,3584]{1,0:T(8,128)(2,1)} %get-tuple-element.72), channel_id=1, source_target_pairs={{0,24},{8,0},{16,8},{24,16},{1,25},{9,1},{17,9},{25,17},{2,26},{10... | collective-permute-start | bytes 688136 | tf_op jit(solution)/shard_map/ppermute | solution.py:32
  359.0 50.1 %collective-permute-start.37 = (bf16[2,256,3584]{2,1,0:T(8,128)(2,1)}, bf16[2,256,3584]{2,1,0:T(8,128)(2,1)}, u32[]{:S(2)}, u32[]{:S(2)}) collective-permute-start(bf16[2,256,3584]{2,1,0:T(8,128)(2,1)} %get-tuple-element.39), channel_id=1, source_target_pairs={{0,1},{1,0},{2,3},{3,2},{4,5},{5,4},{6,7},{7,6},{8,9},{9,8},{10,11... | collective-permute-start | bytes 11010056 | tf_op jit(solution)/shard_map/ppermute | solution.py:32
  360.4 25.1 %collective-permute-start.30 = (bf16[4,2,32,1792]{3,2,0,1:T(8,128)(2,1)S(1)}, bf16[4,2,32,1792]{3,2,0,1:T(8,128)(2,1)S(1)}, u32[]{:S(2)}, u32[]{:S(2)}) collective-permute-start(bf16[4,2,32,1792]{3,2,0,1:T(8,128)(2,1)S(1)} %bitcast.252), channel_id=1, source_target_pairs={{0,4},{4,0},{1,5},{5,1},{2,6},{6,2},{3,7},{7,3},{8,12},{12,8},{9,1... | collective-permute-start | bytes 2752520 | tf_op jit(solution)/shard_map/ppermute | solution.py:32
  361.9 22.5 %collective-permute-start.32 = (bf16[2,4,32,1792]{3,2,1,0:T(8,128)(2,1)S(1)}, bf16[2,4,32,1792]{3,2,1,0:T(8,128)(2,1)S(1)}, u32[]{:S(2)}, u32[]{:S(2)}) collective-permute-start(bf16[2,4,32,1792]{3,2,1,0:T(8,128)(2,1)S(1)} %slice_bitcast_fusion), channel_id=1, source_target_pairs={{0,2},{1,3},{2,0},{3,1},{4,6},{5,7},{6,4},{7,5},{8,10},{9,11},{10,... | collective-permute-start | bytes 2752520 | tf_op jit(solution)/shard_map/ppermute | solution.py:32
  442.1 125.7 %collective-permute-start.34 = (bf16[32,3584]{1,0:T(8,128)(2,1)S(1)}, bf16[32,3584]{1,0:T(8,128)(2,1)S(1)}, u32[]{:S(2)}, u32[]{:S(2)}) collective-permute-start(bf16[32,3584]{1,0:T(8,128)(2,1)S(1)} %get-tuple-element.64), channel_id=1, source_target_pairs={{0,24},{8,0},{16,8},{24,16},{1,25},{9,1},{17,9},{25,17},{2,26},{10... | collective-permute-start | bytes 688136 | tf_op jit(solution)/shard_map/ppermute | solution.py:32
  442.7 125.1 %collective-permute-start.35 = (bf16[32,3584]{1,0:T(8,128)(2,1)S(1)}, bf16[32,3584]{1,0:T(8,128)(2,1)S(1)}, u32[]{:S(2)}, u32[]{:S(2)}) collective-permute-start(bf16[32,3584]{1,0:T(8,128)(2,1)S(1)} %get-tuple-element.65), channel_id=1, source_target_pairs={{0,16},{8,24},{16,0},{24,8},{1,17},{9,25},{17,1},{25,9},{2,18},{10... | collective-permute-start | bytes 688136 | tf_op jit(solution)/shard_map/ppermute | solution.py:32
  444.3 123.6 %collective-permute-start.36 = (bf16[32,3584]{1,0:T(8,128)(2,1)S(1)}, bf16[32,3584]{1,0:T(8,128)(2,1)S(1)}, u32[]{:S(2)}, u32[]{:S(2)}) collective-permute-start(bf16[32,3584]{1,0:T(8,128)(2,1)S(1)} %get-tuple-element.63), channel_id=1, source_target_pairs={{0,8},{8,16},{16,24},{24,0},{1,9},{9,17},{17,25},{25,1},{2,10},{10... | collective-permute-start | bytes 688136 | tf_op jit(solution)/shard_map/ppermute | solution.py:32
  446.6 20.8 %collective-permute-start.43 = (bf16[4,2,32,1792]{3,2,0,1:T(8,128)(2,1)S(1)}, bf16[4,2,32,1792]{3,2,0,1:T(8,128)(2,1)S(1)}, u32[]{:S(2)}, u32[]{:S(2)}) collective-permute-start(bf16[4,2,32,1792]{3,2,0,1:T(8,128)(2,1)S(1)} %bitcast.253), channel_id=1, source_target_pairs={{0,4},{4,0},{1,5},{5,1},{2,6},{6,2},{3,7},{7,3},{8,12},{12,8},{9,1... | collective-permute-start | bytes 2752520 | tf_op jit(solution)/shard_map/ppermute | solution.py:32
  448.1 20.7 %collective-permute-start.44 = (bf16[2,4,32,1792]{3,2,1,0:T(8,128)(2,1)S(1)}, bf16[2,4,32,1792]{3,2,1,0:T(8,128)(2,1)S(1)}, u32[]{:S(2)}, u32[]{:S(2)}) collective-permute-start(bf16[2,4,32,1792]{3,2,1,0:T(8,128)(2,1)S(1)} %dynamic-slice_bitcast_fusion), channel_id=1, source_target_pairs={{0,2},{1,3},{2,0},{3,1},{4,6},{5,7},{6,4},{7,5},{8,10},{9,11},{10,... | collective-permute-start | bytes 2752520 | tf_op jit(solution)/shard_map/ppermute | solution.py:32
  467.4 42.3 %collective-permute-start.39 = (bf16[4,2,32,1792]{3,2,0,1:T(8,128)(2,1)S(1)}, bf16[4,2,32,1792]{3,2,0,1:T(8,128)(2,1)S(1)}, u32[]{:S(2)}, u32[]{:S(2)}) collective-permute-start(bf16[4,2,32,1792]{3,2,0,1:T(8,128)(2,1)S(1)} %bitcast.251), channel_id=1, source_target_pairs={{0,4},{4,0},{1,5},{5,1},{2,6},{6,2},{3,7},{7,3},{8,12},{12,8},{9,1... | collective-permute-start | bytes 2752520 | tf_op jit(solution)/shard_map/ppermute | solution.py:32
  469.0 28.0 %collective-permute-start.46 = (bf16[4,32,1792]{2,1,0:T(8,128)(2,1)S(1)}, bf16[4,32,1792]{2,1,0:T(8,128)(2,1)S(1)}, u32[]{:S(2)}, u32[]{:S(2)}) collective-permute-start(bf16[4,32,1792]{2,1,0:T(8,128)(2,1)S(1)} %slice_bitcast_fusion.4), channel_id=1, source_target_pairs={{0,4},{4,0},{1,5},{5,1},{2,6},{6,2},{3,7},{7,3},{8,12},{12,8},{9,1... | collective-permute-start | bytes 1376264 | tf_op jit(solution)/shard_map/ppermute | solution.py:32
  507.8 20.5 %collective-permute-start.41 = (bf16[2,4,32,1792]{3,2,1,0:T(8,128)(2,1)S(1)}, bf16[2,4,32,1792]{3,2,1,0:T(8,128)(2,1)S(1)}, u32[]{:S(2)}, u32[]{:S(2)}) collective-permute-start(bf16[2,4,32,1792]{3,2,1,0:T(8,128)(2,1)S(1)} %dynamic-slice_bitcast_fusion.1), channel_id=1, source_target_pairs={{0,2},{1,3},{2,0},{3,1},{4,6},{5,7},{6,4},{7,5},{8,10},{9,11},{10,... | collective-permute-start | bytes 2752520 | tf_op jit(solution)/shard_map/ppermute | solution.py:32
  509.6 36.7 %collective-permute-start.47 = (bf16[32,3584]{1,0:T(8,128)(2,1)S(1)}, bf16[32,3584]{1,0:T(8,128)(2,1)S(1)}, u32[]{:S(2)}, u32[]{:S(2)}) collective-permute-start(bf16[32,3584]{1,0:T(8,128)(2,1)S(1)} %get-tuple-element.67), channel_id=1, source_target_pairs={{0,24},{8,0},{16,8},{24,16},{1,25},{9,1},{17,9},{25,17},{2,26},{10... | collective-permute-start | bytes 688136 | tf_op jit(solution)/shard_map/ppermute | solution.py:32
  (34 other events, 469.1 us)
Sparse Core Ops, SparseCore 0:
  10.2 146.6 all-gather.2

commit v4 on v3

--- a/solution.py
+++ b/solution.py
@@ -81,12 +81,9 @@
         out[...] = (v / (1.0 + jnp.exp(-v)) * upper[...]).astype(jnp.bfloat16)
 
 
-def down_body(place, hidden, wd, scale, *outs):
+def down_body(place, hidden, wd, scale, out):
     y = jnp.dot(hidden[...], wd[0], preferred_element_type=jnp.float32)
-    y = (y * scale[...]).astype(jnp.bfloat16)
-    each = y.shape[0] // len(outs)
-    for s, out in enumerate(outs):
-        out[0] = y[s * each : (s + 1) * each]
+    out[0] = (y * scale[...]).astype(jnp.bfloat16)
 
 
 def on_device(tokens, routing, gate_codes, w_gate, w_up, w_down):
@@ -162,28 +159,28 @@
             compiler_params=pltpu.CompilerParams(vmem_limit_bytes=60 * 1024 * 1024),
         )(place, *arrays, w_gate, w_up)
 
-    def out_of(hidden, number):
-        scale = lax.slice_in_dim(walked_scores if number < n_walked else scores, number * rows, (number + 1) * rows, axis=3).reshape(-1, 1)
+    def out_of(hidden, number, s):
+        scale = lax.slice_in_dim(walked_scores if number < n_walked else scores, number * rows, (number + 1) * rows, axis=3)
         return pl.pallas_call(
             down_body,
             grid_spec=pltpu.PrefetchScalarGridSpec(
                 num_scalar_prefetch=1,
                 grid=(steps,),
                 in_specs=[
-                    pl.BlockSpec((tall, hidden_n), lambda k, place: (0, 0)),
+                    pl.BlockSpec((each, hidden_n), lambda k, place: (s, 0)),
                     pl.BlockSpec((1, hidden_n, block), lambda k, place: (0, 0, source(k, place) * per + k % per)),
-                    pl.BlockSpec((tall, 1), lambda k, place: (0, 0)),
+                    pl.BlockSpec((each, 1), lambda k, place: (s, 0)),
                 ],
-                out_specs=[pl.BlockSpec((1, each, block), lambda k, place: (k // per, 0, k % per))] * n_low,
-            ),
-            out_shape=[jax.ShapeDtypeStruct((n_ba, each, width), jnp.bfloat16)] * n_low,
+                out_specs=pl.BlockSpec((1, each, block), lambda k, place: (k // per, 0, k % per)),
+            ),
+            out_shape=jax.ShapeDtypeStruct((n_ba, each, width), jnp.bfloat16),
             cost_estimate=pl.CostEstimate(
-                flops=2 * tall * n_ba * width * hidden_n,
+                flops=2 * each * n_ba * width * hidden_n,
                 transcendentals=0,
-                bytes_accessed=2 * n_ba * width * hidden_n + 2 * tall * n_ba * width,
+                bytes_accessed=2 * n_ba * width * hidden_n + 2 * each * n_ba * width,
             ),
             compiler_params=pltpu.CompilerParams(vmem_limit_bytes=60 * 1024 * 1024),
-        )(place, hidden, w_down, scale)
+        )(place, hidden, w_down, scale.reshape(-1, 1))
 
     def give_back(outs, moving, wait, hold):
         arrived = pair.send(outs)
@@ -240,19 +237,23 @@
         last[number] = next(sums[number])
         return last[number]
 
-    outs = []
+    own_rows = []
     for number in range(n_calls):
-        before = step(number - 3) if number >= 3 else []
+        before = [v for back in (2, 1) if number >= back for v in step(number - back)]
         first, *others = sources[number]
-        first = tie(first, before + outs)
+        first = tie(first, before + own_rows)
         hidden = hidden_of([first] + others, max(number - n_walked, 0))
-        between = [v for back in (3, 2, 1) if number >= back for v in step(number - back)]
-        outs = list(out_of(tie(hidden, between), number))
+        between = [v for back in (2, 1) if number >= back for v in step(number - back)]
+        hidden = tie(hidden, between)
+        outs = [None] * n_low
+        for s in range(1, n_low):
+            outs[s] = out_of(hidden, number, s)
+        outs[0] = out_of(tie(hidden, outs[1:]), number, 0)
+        own_rows = outs[:1]
         sums.append(give_back(outs, number >= n_walked, waits[number], hold))
         step(number)
     end = n_calls - 1
-    waits[end - 1].extend(step(end))
-    for number in (end - 2, end - 1, end, end - 1):
+    for number in (end, end - 1, end):
         step(number)
     hold.extend(step(end))
     for number in range(n_calls):

time: 589 us -> 532 us (0.903)
  the two profiles are of different devices: /device:TPU:0 before, /device:TPU:11 now
where the time goes in v4:
time: 532 us; the launch traced here: 525 us
  waiting for transfers between devices  236 us (44%)
  Pallas kernels  174 us (33%)
  starting transfers between devices  54.4 us (10%)
  other arithmetic  31.9 us (6%)
  between operations  14.1 us (3%)
  local copies, waits for them, and re-layouts  14 us (3%)
    ppermute x53, waiting for transfers between devices, shift(): return lax.ppermute(value, self.axis, pairs)  236 us
    pallas_call x4, Pallas kernels, hidden_of(): pl.pallas_call(functools.partial(hidden_body, steps), grid_spec=pltpu.Pre...  93.9 us
    pallas_call x8, Pallas kernels, out_of(): pl.pallas_call(down_body, grid_spec=pltpu.PrefetchScalarGridSpec(num_scal...  80.5 us
    ppermute x53, starting transfers between devices, shift(): return lax.ppermute(value, self.axis, pairs)  54.4 us
    convert_element_type x24, other arithmetic, total_of(): return total.astype(jnp.bfloat16)  25.1 us
  transfers between devices with their start and end apart: 54, of which 31 were waited for; matrix products, arithmetic and copies ran while one was open for 6% of the time, Pallas kernels for 25%

profile of v4, /device:TPU:11, one launch (start us, length us, event | category | flops | bytes accessed | tf_op | source)
XLA Modules:
  0.0 525.3 jit_solution(6465099706687714140)
XLA Ops:
  16.0 22.0 %collective-permute-done.1 = bf16[32,3584]{1,0:T(8,128)(2,1)S(1)} collective-permute-done((bf16[32,3584]{1,0:T(8,128)(2,1)S(1)}, bf16[32,3584]{1,0:T(8,128)(2,1)S(1)}, u32[]{:S(2)}, u32[]{:S(2)}) %collective-permute-start.1) | collective-permute-done | bytes 229408 | tf_op jit(solution)/shard_map/ppermute | solution.py:32
  38.1 4.4 collective-permute-done.2
  44.4 14.6 %collective-permute-done.5 = bf16[4,32,1792]{2,1,0:T(8,128)(2,1)S(1)} collective-permute-done((bf16[4,32,1792]{2,1,0:T(8,128)(2,1)S(1)}, bf16[4,32,1792]{2,1,0:T(8,128)(2,1)S(1)}, u32[]{:S(2)}, u32[]{:S(2)}) %collective-permute-start.5) | collective-permute-done | bytes 458784 | tf_op jit(solution)/shard_map/ppermute | solution.py:32
  61.9 26.3 %collective-permute-done.6 = bf16[2,4,32,1792]{3,2,1,0:T(8,128)(2,1)S(1)} collective-permute-done((bf16[2,4,32,1792]{3,2,1,0:T(8,128)(2,1)S(1)}, bf16[2,4,32,1792]{3,2,1,0:T(8,128)(2,1)S(1)}, u32[]{:S(2)}, u32[]{:S(2)}) %collective-permute-start.6) | collective-permute-done | bytes 917536 | tf_op jit(solution)/shard_map/ppermute | solution.py:32
  110.1 28.1 %collective-permute-done.22 = bf16[32,3584]{1,0:T(8,128)(2,1)S(1)} collective-permute-done((bf16[32,3584]{1,0:T(8,128)(2,1)S(1)}, bf16[32,3584]{1,0:T(8,128)(2,1)S(1)}, u32[]{:S(2)}, u32[]{:S(2)}) %collective-permute-start.22) | collective-permute-done | bytes 229408 | tf_op jit(solution)/shard_map/ppermute | solution.py:32
  138.2 4.7 collective-permute-done.23
  143.5 23.9 %shard_map.64.hidden = bf16[512,1024]{1,0:T(8,128)(2,1)} custom-call(s32[2]{0:T(128)} %pad_add_fusion.place, bf16[2,4,2,32,3584]{4,3,2,1,0:T(8,128)(2,1)} %maximum_maximum_fusion.refs_0_, bf16[2,4,2,32,3584]{4,3,2,1,0:T(8,128)(2,1)} %collective-permute-done.7.refs_1_, bf16[1,7168,1024]{2,1,0:T(8,128)(2,1)} %refs_2_.7, bf16[1,7168,1024]{2,1,0:T(8,128)(2,1)} %refs_3_.7), custom_call_target="tpu_custom_call" | custom-call | flops 15032385536 | bytes 36700160 | tf_op jit(solution)/shard_map/pallas_call | solution.py:144
  167.4 10.0 %shard_map.65 = bf16[2,256,3584]{2,1,0:T(8,128)(2,1)} custom-call(s32[2]{0:T(128)} %pad_add_fusion.place, bf16[512,1024]{1,0:T(8,128)(2,1)} %shard_map.64.hidden, bf16[1,1024,7168]{2,1,0:T(8,128)(2,1)} %wd.15, f32[512,1]{1,0:T(8,128)} %reshape.233.scale), custom_call_target="tpu_custom_call" | custom-call | flops 3758096384 | bytes 18350080 | tf_op jit(solution)/shard_map/pallas_call | solution.py:164
  180.4 10.4 %collective-permute-done.26 = bf16[4,32,1792]{2,1,0:T(8,128)(2,1)S(1)} collective-permute-done((bf16[4,32,1792]{2,1,0:T(8,128)(2,1)S(1)}, bf16[4,32,1792]{2,1,0:T(8,128)(2,1)S(1)}, u32[]{:S(2)}, u32[]{:S(2)}) %collective-permute-start.26) | collective-permute-done | bytes 458784 | tf_op jit(solution)/shard_map/ppermute | solution.py:32
  192.3 18.2 %collective-permute-done.25 = bf16[4,2,32,1792]{3,2,0,1:T(8,128)(2,1)S(1)} collective-permute-done((bf16[4,2,32,1792]{3,2,0,1:T(8,128)(2,1)S(1)}, bf16[4,2,32,1792]{3,2,0,1:T(8,128)(2,1)S(1)}, u32[]{:S(2)}, u32[]{:S(2)}) %collective-permute-start.25) | collective-permute-done | bytes 917536 | tf_op jit(solution)/shard_map/ppermute | solution.py:32
  216.8 10.0 %shard_map.66 = bf16[2,256,3584]{2,1,0:T(8,128)(2,1)} custom-call(s32[2]{0:T(128)} %pad_add_fusion.place, bf16[512,1024]{1,0:T(8,128)(2,1)} %shard_map.64.hidden, bf16[1,1024,7168]{2,1,0:T(8,128)(2,1)} %wd.15, f32[512,1]{1,0:T(8,128)} %reshape.233.scale), custom_call_target="tpu_custom_call" | custom-call | flops 3758096384 | bytes 18350080 | tf_op jit(solution)/shard_map/pallas_call | solution.py:164
  226.7 4.0 add_convert_fusion.3
  235.4 23.2 %shard_map.67.hidden = bf16[512,1024]{1,0:T(8,128)(2,1)} custom-call(s32[2]{0:T(128)} %pad_add_fusion.place, bf16[2,4,2,32,3584]{4,3,2,1,0:T(8,128)(2,1)} %maximum_maximum_fusion.1.refs_0_, bf16[2,4,2,32,3584]{4,3,2,1,0:T(8,128)(2,1)} %collective-permute-done.28.refs_1_, bf16[1,7168,1024]{2,1,0:T(8,128)(2,1)} %refs_2_.7, bf16[1,7168,1024]{2,1,0:T(8,128)(2,1)} %refs_3_.7), custom_call_target="tpu_custom_call" | custom-call | flops 15032385536 | bytes 36700160 | tf_op jit(solution)/shard_map/pallas_call | solution.py:144
  262.6 10.3 %shard_map.68 = bf16[2,256,3584]{2,1,0:T(8,128)(2,1)} custom-call(s32[2]{0:T(128)} %pad_add_fusion.place, bf16[512,1024]{1,0:T(8,128)(2,1)} %shard_map.67.hidden, bf16[1,1024,7168]{2,1,0:T(8,128)(2,1)} %wd.15, f32[512,1]{1,0:T(8,128)} %reshape.234.scale), custom_call_target="tpu_custom_call" | custom-call | flops 3758096384 | bytes 18350080 | tf_op jit(solution)/shard_map/pallas_call | solution.py:164
  277.5 10.0 %shard_map.69 = bf16[2,256,3584]{2,1,0:T(8,128)(2,1)} custom-call(s32[2]{0:T(128)} %pad_add_fusion.place, bf16[512,1024]{1,0:T(8,128)(2,1)} %shard_map.67.hidden, bf16[1,1024,7168]{2,1,0:T(8,128)(2,1)} %wd.15, f32[512,1]{1,0:T(8,128)} %reshape.234.scale), custom_call_target="tpu_custom_call" | custom-call | flops 3758096384 | bytes 18350080 | tf_op jit(solution)/shard_map/pallas_call | solution.py:164
  296.1 8.1 %collective-permute-done.19 = bf16[32,3584]{1,0:T(8,128)(2,1)S(1)} collective-permute-done((bf16[32,3584]{1,0:T(8,128)(2,1)S(1)}, bf16[32,3584]{1,0:T(8,128)(2,1)S(1)}, u32[]{:S(2)}, u32[]{:S(2)}) %collective-permute-start.19) | collective-permute-done | bytes 229408 | tf_op jit(solution)/shard_map/ppermute | solution.py:32
  304.2 4.9 collective-permute-done.20
  309.2 6.0 %collective-permute-done.32 = bf16[2,4,32,1792]{3,2,1,0:T(8,128)(2,1)S(1)} collective-permute-done((bf16[2,4,32,1792]{3,2,1,0:T(8,128)(2,1)S(1)}, bf16[2,4,32,1792]{3,2,1,0:T(8,128)(2,1)S(1)}, u32[]{:S(2)}, u32[]{:S(2)}) %collective-permute-start.32) | collective-permute-done | bytes 917536 | tf_op jit(solution)/shard_map/ppermute | solution.py:32
  315.7 23.4 %shard_map.70.hidden = bf16[512,1024]{1,0:T(8,128)(2,1)} custom-call(s32[2]{0:T(128)} %pad_add_fusion.place, bf16[4,2,2,2,64,3584]{5,4,3,2,1,0:T(8,128)(2,1)} %bitcast.234, bf16[4,2,2,2,64,3584]{5,4,3,2,1,0:T(8,128)(2,1)} %bitcast.235, bf16[1,7168,1024]{2,1,0:T(8,128)(2,1)} %refs_2_.7, bf16[1,7168,1024]{2,1,0:T(8,128)(2,1)} %refs_3_.7), custom_call_target="tpu_custom_call" | custom-call | flops 15032385536 | bytes 36700160 | tf_op jit(solution)/shard_map/pallas_call | solution.py:144
  339.1 10.0 %shard_map.71 = bf16[2,256,3584]{2,1,0:T(8,128)(2,1)} custom-call(s32[2]{0:T(128)} %pad_add_fusion.place, bf16[512,1024]{1,0:T(8,128)(2,1)} %shard_map.70.hidden, bf16[1,1024,7168]{2,1,0:T(8,128)(2,1)} %wd.15, f32[512,1]{1,0:T(8,128)} %reshape.235.scale), custom_call_target="tpu_custom_call" | custom-call | flops 3758096384 | bytes 18350080 | tf_op jit(solution)/shard_map/pallas_call | solution.py:164
  353.9 10.5 %collective-permute-done.33 = bf16[4,32,1792]{2,1,0:T(8,128)(2,1)S(1)} collective-permute-done((bf16[4,32,1792]{2,1,0:T(8,128)(2,1)S(1)}, bf16[4,32,1792]{2,1,0:T(8,128)(2,1)S(1)}, u32[]{:S(2)}, u32[]{:S(2)}) %collective-permute-start.33) | collective-permute-done | bytes 458784 | tf_op jit(solution)/shard_map/ppermute | solution.py:32
  370.7 10.3 %collective-permute-done.35 = bf16[32,3584]{1,0:T(8,128)(2,1)S(1)} collective-permute-done((bf16[32,3584]{1,0:T(8,128)(2,1)S(1)}, bf16[32,3584]{1,0:T(8,128)(2,1)S(1)}, u32[]{:S(2)}, u32[]{:S(2)}) %collective-permute-start.35) | collective-permute-done | bytes 229408 | tf_op jit(solution)/shard_map/ppermute | solution.py:32
  381.0 4.9 collective-permute-done.36
  386.0 10.2 %shard_map.72 = bf16[2,256,3584]{2,1,0:T(8,128)(2,1)} custom-call(s32[2]{0:T(128)} %pad_add_fusion.place, bf16[512,1024]{1,0:T(8,128)(2,1)} %shard_map.70.hidden, bf16[1,1024,7168]{2,1,0:T(8,128)(2,1)} %wd.15, f32[512,1]{1,0:T(8,128)} %reshape.235.scale), custom_call_target="tpu_custom_call" | custom-call | flops 3758096384 | bytes 18350080 | tf_op jit(solution)/shard_map/pallas_call | solution.py:164
  404.1 23.4 %shard_map.73.hidden = bf16[512,1024]{1,0:T(8,128)(2,1)} custom-call(s32[2]{0:T(128)} %pad_add_fusion.place, bf16[4,2,2,2,64,3584]{5,4,3,2,1,0:T(8,128)(2,1)} %bitcast.236, bf16[4,2,2,2,64,3584]{5,4,3,2,1,0:T(8,128)(2,1)} %bitcast.237, bf16[1,7168,1024]{2,1,0:T(8,128)(2,1)} %refs_2_.7, bf16[1,7168,1024]{2,1,0:T(8,128)(2,1)} %refs_3_.7), custom_call_target="tpu_custom_call" | custom-call | flops 15032385536 | bytes 36700160 | tf_op jit(solution)/shard_map/pallas_call | solution.py:144
  430.3 10.0 %shard_map.74 = bf16[2,256,3584]{2,1,0:T(8,128)(2,1)} custom-call(s32[2]{0:T(128)} %pad_add_fusion.place, bf16[512,1024]{1,0:T(8,128)(2,1)} %shard_map.73.hidden, bf16[1,1024,7168]{2,1,0:T(8,128)(2,1)} %wd.15, f32[512,1]{1,0:T(8,128)} %reshape.236.scale), custom_call_target="tpu_custom_call" | custom-call | flops 3758096384 | bytes 18350080 | tf_op jit(solution)/shard_map/pallas_call | solution.py:164
  442.9 10.0 %shard_map.75 = bf16[2,256,3584]{2,1,0:T(8,128)(2,1)} custom-call(s32[2]{0:T(128)} %pad_add_fusion.place, bf16[512,1024]{1,0:T(8,128)(2,1)} %shard_map.73.hidden, bf16[1,1024,7168]{2,1,0:T(8,128)(2,1)} %wd.15, f32[512,1]{1,0:T(8,128)} %reshape.236.scale), custom_call_target="tpu_custom_call" | custom-call | flops 3758096384 | bytes 18350080 | tf_op jit(solution)/shard_map/pallas_call | solution.py:164
  455.7 4.0 add_convert_fusion
  465.4 15.6 %collective-permute-done.48 = bf16[2,4,32,1792]{3,2,1,0:T(8,128)(2,1)S(1)} collective-permute-done((bf16[2,4,32,1792]{3,2,1,0:T(8,128)(2,1)S(1)}, bf16[2,4,32,1792]{3,2,1,0:T(8,128)(2,1)S(1)}, u32[]{:S(2)}, u32[]{:S(2)}) %collective-permute-start.48) | collective-permute-done | bytes 917536 | tf_op jit(solution)/shard_map/ppermute | solution.py:32
  485.7 9.1 %collective-permute-done.49 = bf16[4,32,1792]{2,1,0:T(8,128)(2,1)S(1)} collective-permute-done((bf16[4,32,1792]{2,1,0:T(8,128)(2,1)S(1)}, bf16[4,32,1792]{2,1,0:T(8,128)(2,1)S(1)}, u32[]{:S(2)}, u32[]{:S(2)}) %collective-permute-start.49) | collective-permute-done | bytes 458784 | tf_op jit(solution)/shard_map/ppermute | solution.py:32
  500.1 12.1 %collective-permute-done.51 = bf16[32,3584]{1,0:T(8,128)(2,1)S(1)} collective-permute-done((bf16[32,3584]{1,0:T(8,128)(2,1)S(1)}, bf16[32,3584]{1,0:T(8,128)(2,1)S(1)}, u32[]{:S(2)}, u32[]{:S(2)}) %collective-permute-start.51) | collective-permute-done | bytes 229408 | tf_op jit(solution)/shard_map/ppermute | solution.py:32
  512.2 4.9 collective-permute-done.52
  (188 shorter events, 113.5 us)
Async XLA Ops:
  6.5 309.2 %all-gather.3.cloned.1.call-start = ((), (), s32[]{:S(2)}) async-start(), calls=%async_computation | async-start | bytes 15138816 | tf_op jit(solution)/shard_map/all_gather | solution.py:225
  10.8 27.2 %collective-permute-start.1 = (bf16[32,3584]{1,0:T(8,128)(2,1)S(1)}, bf16[32,3584]{1,0:T(8,128)(2,1)S(1)}, u32[]{:S(2)}, u32[]{:S(2)}) collective-permute-start(bf16[32,3584]{1,0:T(8,128)(2,1)S(1)} %get-tuple-element.67), channel_id=1, source_target_pairs={{0,16},{8,24},{16,0},{24,8},{1,17},{9,25},{17,1},{25,9},{2,18},{10... | collective-permute-start | bytes 688136 | tf_op jit(solution)/shard_map/ppermute | solution.py:32
  11.9 30.6 %collective-permute-start.2 = (bf16[32,3584]{1,0:T(8,128)(2,1)S(1)}, bf16[32,3584]{1,0:T(8,128)(2,1)S(1)}, u32[]{:S(2)}, u32[]{:S(2)}) collective-permute-start(bf16[32,3584]{1,0:T(8,128)(2,1)S(1)} %get-tuple-element.67), channel_id=1, source_target_pairs={{0,24},{8,0},{16,8},{24,16},{1,25},{9,1},{17,9},{25,17},{2,26},{10... | collective-permute-start | bytes 688136 | tf_op jit(solution)/shard_map/ppermute | solution.py:32
  44.1 17.6 %collective-permute-start.3 = (bf16[4,32,1792]{2,1,0:T(8,128)(2,1)S(1)}, bf16[4,32,1792]{2,1,0:T(8,128)(2,1)S(1)}, u32[]{:S(2)}, u32[]{:S(2)}) collective-permute-start(bf16[4,32,1792]{2,1,0:T(8,128)(2,1)S(1)} %get-tuple-element.62), channel_id=1, source_target_pairs={{0,2},{1,3},{2,0},{3,1},{4,6},{5,7},{6,4},{7,5},{8,10},{9,11},{10,... | collective-permute-start | bytes 1376264 | tf_op jit(solution)/shard_map/ppermute | solution.py:32
  59.1 29.2 %collective-permute-start.6 = (bf16[2,4,32,1792]{3,2,1,0:T(8,128)(2,1)S(1)}, bf16[2,4,32,1792]{3,2,1,0:T(8,128)(2,1)S(1)}, u32[]{:S(2)}, u32[]{:S(2)}) collective-permute-start(bf16[2,4,32,1792]{3,2,1,0:T(8,128)(2,1)S(1)} %get-tuple-element.64), channel_id=1, source_target_pairs={{0,2},{1,3},{2,0},{3,1},{4,6},{5,7},{6,4},{7,5},{8,10},{9,11},{10,... | collective-permute-start | bytes 2752520 | tf_op jit(solution)/shard_map/ppermute | solution.py:32
  61.9 26.4 %collective-permute-start.4 = (bf16[4,2,32,1792]{3,2,0,1:T(8,128)(2,1)S(1)}, bf16[4,2,32,1792]{3,2,0,1:T(8,128)(2,1)S(1)}, u32[]{:S(2)}, u32[]{:S(2)}) collective-permute-start(bf16[4,2,32,1792]{3,2,0,1:T(8,128)(2,1)S(1)} %get-tuple-element.58), channel_id=1, source_target_pairs={{0,4},{4,0},{1,5},{5,1},{2,6},{6,2},{3,7},{7,3},{8,12},{12,8},{9,1... | collective-permute-start | bytes 2752520 | tf_op jit(solution)/shard_map/ppermute | solution.py:32
  90.2 53.3 %collective-permute-start.7 = (bf16[2,4,2,32,3584]{4,3,2,1,0:T(8,128)(2,1)}, bf16[2,4,2,32,3584]{4,3,2,1,0:T(8,128)(2,1)}, u32[]{:S(2)}, u32[]{:S(2)}) collective-permute-start(bf16[2,4,2,32,3584]{4,3,2,1,0:T(8,128)(2,1)} %maximum_maximum_fusion.refs_0_), channel_id=1, source_target_pairs={{0,1},{1,0},{2,3},{3,2},{4,5},{5,4},{6,7},{7,6},{8,9},{9,8},{10,11... | collective-permute-start | bytes 11010056 | tf_op jit(solution)/shard_map/ppermute | solution.py:32
  94.0 16.1 %collective-permute-start.21 = (bf16[32,3584]{1,0:T(8,128)(2,1)S(1)}, bf16[32,3584]{1,0:T(8,128)(2,1)S(1)}, u32[]{:S(2)}, u32[]{:S(2)}) collective-permute-start(bf16[32,3584]{1,0:T(8,128)(2,1)S(1)} %get-tuple-element.68), channel_id=1, source_target_pairs={{0,8},{8,16},{16,24},{24,0},{1,9},{9,17},{17,25},{25,1},{2,10},{10... | collective-permute-start | bytes 688136 | tf_op jit(solution)/shard_map/ppermute | solution.py:32
  95.7 42.5 %collective-permute-start.22 = (bf16[32,3584]{1,0:T(8,128)(2,1)S(1)}, bf16[32,3584]{1,0:T(8,128)(2,1)S(1)}, u32[]{:S(2)}, u32[]{:S(2)}) collective-permute-start(bf16[32,3584]{1,0:T(8,128)(2,1)S(1)} %get-tuple-element.68), channel_id=1, source_target_pairs={{0,16},{8,24},{16,0},{24,8},{1,17},{9,25},{17,1},{25,9},{2,18},{10... | collective-permute-start | bytes 688136 | tf_op jit(solution)/shard_map/ppermute | solution.py:32
  98.2 44.6 %collective-permute-start.23 = (bf16[32,3584]{1,0:T(8,128)(2,1)S(1)}, bf16[32,3584]{1,0:T(8,128)(2,1)S(1)}, u32[]{:S(2)}, u32[]{:S(2)}) collective-permute-start(bf16[32,3584]{1,0:T(8,128)(2,1)S(1)} %get-tuple-element.68), channel_id=1, source_target_pairs={{0,24},{8,0},{16,8},{24,16},{1,25},{9,1},{17,9},{25,17},{2,26},{10... | collective-permute-start | bytes 688136 | tf_op jit(solution)/shard_map/ppermute | solution.py:32
  143.2 35.6 %collective-permute-start.24 = (bf16[4,32,1792]{2,1,0:T(8,128)(2,1)S(1)}, bf16[4,32,1792]{2,1,0:T(8,128)(2,1)S(1)}, u32[]{:S(2)}, u32[]{:S(2)}) collective-permute-start(bf16[4,32,1792]{2,1,0:T(8,128)(2,1)S(1)} %get-tuple-element.74), channel_id=1, source_target_pairs={{0,2},{1,3},{2,0},{3,1},{4,6},{5,7},{6,4},{7,5},{8,10},{9,11},{10,... | collective-permute-start | bytes 1376264 | tf_op jit(solution)/shard_map/ppermute | solution.py:32
  177.4 49.4 %collective-permute-start.13 = (bf16[2,256,3584]{2,1,0:T(8,128)(2,1)}, bf16[2,256,3584]{2,1,0:T(8,128)(2,1)}, u32[]{:S(2)}, u32[]{:S(2)}) collective-permute-start(bf16[2,256,3584]{2,1,0:T(8,128)(2,1)} %shard_map.65), channel_id=1, source_target_pairs={{0,1},{1,0},{2,3},{3,2},{4,5},{5,4},{6,7},{7,6},{8,9},{9,8},{10,11... | collective-permute-start | bytes 11010056 | tf_op jit(solution)/shard_map/ppermute | solution.py:32
  178.9 31.6 %collective-permute-start.25 = (bf16[4,2,32,1792]{3,2,0,1:T(8,128)(2,1)S(1)}, bf16[4,2,32,1792]{3,2,0,1:T(8,128)(2,1)S(1)}, u32[]{:S(2)}, u32[]{:S(2)}) collective-permute-start(bf16[4,2,32,1792]{3,2,0,1:T(8,128)(2,1)S(1)} %get-tuple-element.70), channel_id=1, source_target_pairs={{0,4},{4,0},{1,5},{5,1},{2,6},{6,2},{3,7},{7,3},{8,12},{12,8},{9,1... | collective-permute-start | bytes 2752520 | tf_op jit(solution)/shard_map/ppermute | solution.py:32
  191.0 20.7 %collective-permute-start.27 = (bf16[2,4,32,1792]{3,2,1,0:T(8,128)(2,1)S(1)}, bf16[2,4,32,1792]{3,2,1,0:T(8,128)(2,1)S(1)}, u32[]{:S(2)}, u32[]{:S(2)}) collective-permute-start(bf16[2,4,32,1792]{3,2,1,0:T(8,128)(2,1)S(1)} %get-tuple-element.76), channel_id=1, source_target_pairs={{0,2},{1,3},{2,0},{3,1},{4,6},{5,7},{6,4},{7,5},{8,10},{9,11},{10,... | collective-permute-start | bytes 2752520 | tf_op jit(solution)/shard_map/ppermute | solution.py:32
  213.5 21.8 %collective-permute-start.28 = (bf16[2,4,2,32,3584]{4,3,2,1,0:T(8,128)(2,1)}, bf16[2,4,2,32,3584]{4,3,2,1,0:T(8,128)(2,1)}, u32[]{:S(2)}, u32[]{:S(2)}) collective-permute-start(bf16[2,4,2,32,3584]{4,3,2,1,0:T(8,128)(2,1)} %maximum_maximum_fusion.1.refs_0_), channel_id=1, source_target_pairs={{0,1},{1,0},{2,3},{3,2},{4,5},{5,4},{6,7},{7,6},{8,9},{9,8},{10,11... | collective-permute-start | bytes 11010056 | tf_op jit(solution)/shard_map/ppermute | solution.py:32
  231.8 26.8 %collective-permute-start.16 = (bf16[2,4,32,1792]{3,2,1,0:T(8,128)(2,1)}, bf16[2,4,32,1792]{3,2,1,0:T(8,128)(2,1)}, u32[]{:S(2)}, u32[]{:S(2)}) collective-permute-start(bf16[2,4,32,1792]{3,2,1,0:T(8,128)(2,1)} %slice_bitcast_fusion.2), channel_id=1, source_target_pairs={{0,2},{1,3},{2,0},{3,1},{4,6},{5,7},{6,4},{7,5},{8,10},{9,11},{10,... | collective-permute-start | bytes 2752520 | tf_op jit(solution)/shard_map/ppermute | solution.py:32
  235.1 25.9 %collective-permute-start.14 = (bf16[4,2,32,1792]{3,2,0,1:T(8,128)(2,1)}, bf16[4,2,32,1792]{3,2,0,1:T(8,128)(2,1)}, u32[]{:S(2)}, u32[]{:S(2)}) collective-permute-start(bf16[4,2,32,1792]{3,2,0,1:T(8,128)(2,1)} %bitcast.232), channel_id=1, source_target_pairs={{0,4},{4,0},{1,5},{5,1},{2,6},{6,2},{3,7},{7,3},{8,12},{12,8},{9,1... | collective-permute-start | bytes 2752520 | tf_op jit(solution)/shard_map/ppermute | solution.py:32
  272.9 19.2 %collective-permute-start.29 = (bf16[2,256,3584]{2,1,0:T(8,128)(2,1)}, bf16[2,256,3584]{2,1,0:T(8,128)(2,1)}, u32[]{:S(2)}, u32[]{:S(2)}) collective-permute-start(bf16[2,256,3584]{2,1,0:T(8,128)(2,1)} %shard_map.68), channel_id=1, source_target_pairs={{0,1},{1,0},{2,3},{3,2},{4,5},{5,4},{6,7},{7,6},{8,9},{9,8},{10,11... | collective-permute-start | bytes 11010056 | tf_op jit(solution)/shard_map/ppermute | solution.py:32
  289.8 19.3 %collective-permute-start.20 = (bf16[32,3584]{1,0:T(8,128)(2,1)S(1)}, bf16[32,3584]{1,0:T(8,128)(2,1)S(1)}, u32[]{:S(2)}, u32[]{:S(2)}) collective-permute-start(bf16[32,3584]{1,0:T(8,128)(2,1)S(1)} %get-tuple-element.56), channel_id=1, source_target_pairs={{0,8},{8,16},{16,24},{24,0},{1,9},{9,17},{17,25},{25,1},{2,10},{10... | collective-permute-start | bytes 688136 | tf_op jit(solution)/shard_map/ppermute | solution.py:32
  295.3 20.0 %collective-permute-start.32 = (bf16[2,4,32,1792]{3,2,1,0:T(8,128)(2,1)S(1)}, bf16[2,4,32,1792]{3,2,1,0:T(8,128)(2,1)S(1)}, u32[]{:S(2)}, u32[]{:S(2)}) collective-permute-start(bf16[2,4,32,1792]{3,2,1,0:T(8,128)(2,1)S(1)} %slice_bitcast_fusion), channel_id=1, source_target_pairs={{0,2},{1,3},{2,0},{3,1},{4,6},{5,7},{6,4},{7,5},{8,10},{9,11},{10,... | collective-permute-start | bytes 2752520 | tf_op jit(solution)/shard_map/ppermute | solution.py:32
  295.7 19.8 %collective-permute-start.30 = (bf16[4,2,32,1792]{3,2,0,1:T(8,128)(2,1)S(1)}, bf16[4,2,32,1792]{3,2,0,1:T(8,128)(2,1)S(1)}, u32[]{:S(2)}, u32[]{:S(2)}) collective-permute-start(bf16[4,2,32,1792]{3,2,0,1:T(8,128)(2,1)S(1)} %bitcast.252), channel_id=1, source_target_pairs={{0,4},{4,0},{1,5},{5,1},{2,6},{6,2},{3,7},{7,3},{8,12},{12,8},{9,1... | collective-permute-start | bytes 2752520 | tf_op jit(solution)/shard_map/ppermute | solution.py:32
  349.2 47.1 %collective-permute-start.37 = (bf16[2,256,3584]{2,1,0:T(8,128)(2,1)}, bf16[2,256,3584]{2,1,0:T(8,128)(2,1)}, u32[]{:S(2)}, u32[]{:S(2)}) collective-permute-start(bf16[2,256,3584]{2,1,0:T(8,128)(2,1)} %shard_map.71), channel_id=1, source_target_pairs={{0,1},{1,0},{2,3},{3,2},{4,5},{5,4},{6,7},{7,6},{8,9},{9,8},{10,11... | collective-permute-start | bytes 11010056 | tf_op jit(solution)/shard_map/ppermute | solution.py:32
  364.7 16.3 %collective-permute-start.35 = (bf16[32,3584]{1,0:T(8,128)(2,1)S(1)}, bf16[32,3584]{1,0:T(8,128)(2,1)S(1)}, u32[]{:S(2)}, u32[]{:S(2)}) collective-permute-start(bf16[32,3584]{1,0:T(8,128)(2,1)S(1)} %get-tuple-element.52), channel_id=1, source_target_pairs={{0,16},{8,24},{16,0},{24,8},{1,17},{9,25},{17,1},{25,9},{2,18},{10... | collective-permute-start | bytes 688136 | tf_op jit(solution)/shard_map/ppermute | solution.py:32
  366.6 19.3 %collective-permute-start.36 = (bf16[32,3584]{1,0:T(8,128)(2,1)S(1)}, bf16[32,3584]{1,0:T(8,128)(2,1)S(1)}, u32[]{:S(2)}, u32[]{:S(2)}) collective-permute-start(bf16[32,3584]{1,0:T(8,128)(2,1)S(1)} %get-tuple-element.53), channel_id=1, source_target_pairs={{0,8},{8,16},{16,24},{24,0},{1,9},{9,17},{17,25},{25,1},{2,10},{10... | collective-permute-start | bytes 688136 | tf_op jit(solution)/shard_map/ppermute | solution.py:32
  400.7 26.8 %collective-permute-start.40 = (bf16[2,4,32,1792]{3,2,1,0:T(8,128)(2,1)S(1)}, bf16[2,4,32,1792]{3,2,1,0:T(8,128)(2,1)}, u32[]{:S(2)}, u32[]{:S(2)}) collective-permute-start(bf16[2,4,32,1792]{3,2,1,0:T(8,128)(2,1)S(1)} %dynamic-slice_bitcast_fusion.1), channel_id=1, source_target_pairs={{0,2},{1,3},{2,0},{3,1},{4,6},{5,7},{6,4},{7,5},{8,10},{9,11},{10,... | collective-permute-start | bytes 2752520 | tf_op jit(solution)/shard_map/ppermute | solution.py:32
  402.9 25.9 %collective-permute-start.38 = (bf16[4,2,32,1792]{3,2,0,1:T(8,128)(2,1)}, bf16[4,2,32,1792]{3,2,0,1:T(8,128)(2,1)}, u32[]{:S(2)}, u32[]{:S(2)}) collective-permute-start(bf16[4,2,32,1792]{3,2,0,1:T(8,128)(2,1)} %bitcast.230), channel_id=1, source_target_pairs={{0,4},{4,0},{1,5},{5,1},{2,6},{6,2},{3,7},{7,3},{8,12},{12,8},{9,1... | collective-permute-start | bytes 2752520 | tf_op jit(solution)/shard_map/ppermute | solution.py:32
  460.0 20.9 %collective-permute-start.48 = (bf16[2,4,32,1792]{3,2,1,0:T(8,128)(2,1)S(1)}, bf16[2,4,32,1792]{3,2,1,0:T(8,128)(2,1)S(1)}, u32[]{:S(2)}, u32[]{:S(2)}) collective-permute-start(bf16[2,4,32,1792]{3,2,1,0:T(8,128)(2,1)S(1)} %dynamic-slice_bitcast_fusion), channel_id=1, source_target_pairs={{0,2},{1,3},{2,0},{3,1},{4,6},{5,7},{6,4},{7,5},{8,10},{9,11},{10,... | collective-permute-start | bytes 2752520 | tf_op jit(solution)/shard_map/ppermute | solution.py:32
  461.3 33.8 %collective-permute-start.42 = (bf16[32,3584]{1,0:T(8,128)(2,1)S(1)}, bf16[32,3584]{1,0:T(8,128)(2,1)S(1)}, u32[]{:S(2)}, u32[]{:S(2)}) collective-permute-start(bf16[32,3584]{1,0:T(8,128)(2,1)S(1)} %get-tuple-element.46), channel_id=1, source_target_pairs={{0,24},{8,0},{16,8},{24,16},{1,25},{9,1},{17,9},{25,17},{2,26},{10... | collective-permute-start | bytes 688136 | tf_op jit(solution)/shard_map/ppermute | solution.py:32
  462.7 32.4 %collective-permute-start.43 = (bf16[32,3584]{1,0:T(8,128)(2,1)S(1)}, bf16[32,3584]{1,0:T(8,128)(2,1)S(1)}, u32[]{:S(2)}, u32[]{:S(2)}) collective-permute-start(bf16[32,3584]{1,0:T(8,128)(2,1)S(1)} %get-tuple-element.47), channel_id=1, source_target_pairs={{0,16},{8,24},{16,0},{24,8},{1,17},{9,25},{17,1},{25,9},{2,18},{10... | collective-permute-start | bytes 688136 | tf_op jit(solution)/shard_map/ppermute | solution.py:32
  464.7 30.4 %collective-permute-start.44 = (bf16[32,3584]{1,0:T(8,128)(2,1)S(1)}, bf16[32,3584]{1,0:T(8,128)(2,1)S(1)}, u32[]{:S(2)}, u32[]{:S(2)}) collective-permute-start(bf16[32,3584]{1,0:T(8,128)(2,1)S(1)} %get-tuple-element.45), channel_id=1, source_target_pairs={{0,8},{8,16},{16,24},{24,0},{1,9},{9,17},{17,25},{25,1},{2,10},{10... | collective-permute-start | bytes 688136 | tf_op jit(solution)/shard_map/ppermute | solution.py:32
  465.0 20.0 %collective-permute-start.46 = (bf16[4,2,32,1792]{3,2,0,1:T(8,128)(2,1)S(1)}, bf16[4,2,32,1792]{3,2,0,1:T(8,128)(2,1)S(1)}, u32[]{:S(2)}, u32[]{:S(2)}) collective-permute-start(bf16[4,2,32,1792]{3,2,0,1:T(8,128)(2,1)S(1)} %bitcast.253), channel_id=1, source_target_pairs={{0,4},{4,0},{1,5},{5,1},{2,6},{6,2},{3,7},{7,3},{8,12},{12,8},{9,1... | collective-permute-start | bytes 2752520 | tf_op jit(solution)/shard_map/ppermute | solution.py:32
  497.6 19.5 %collective-permute-start.52 = (bf16[32,3584]{1,0:T(8,128)(2,1)S(1)}, bf16[32,3584]{1,0:T(8,128)(2,1)S(1)}, u32[]{:S(2)}, u32[]{:S(2)}) collective-permute-start(bf16[32,3584]{1,0:T(8,128)(2,1)S(1)} %get-tuple-element.48), channel_id=1, source_target_pairs={{0,8},{8,16},{16,24},{24,0},{1,9},{9,17},{17,25},{25,1},{2,10},{10... | collective-permute-start | bytes 688136 | tf_op jit(solution)/shard_map/ppermute | solution.py:32
  (26 other events, 242.8 us)
Sparse Core Ops, SparseCore 0:
  10.2 140.0 all-gather.2
